TPU v7x, 32 devices: a whole 2x2x4 slice. The times are simulated.
32 devices in a mesh: net: 4 (over x, core), rep: 8 (over z, y).
Axes of the slice: x: 2, y: 2, z: 4, core: 2. Of those that a mesh axis runs over, the one named last changes fastest.
Arguments:
- latent: bfloat16 [32, 64, 256], P('net', 'rep'), may hold values from -7.2 to 7.2
- hint: bfloat16 [32, 64, 64, 192], P('net', 'rep'), may hold values from -6 to 6
- cond_ids: int32 [32, 1], P('net'), may hold values from 0 to 3; in each aligned block of 8 rows (0 to 7, 8 to 15, ...) at most 4 rows name the same one
- valid: int32 [32], P('net'), may hold values 0 or 1
- cond_scale: float32 [32], P('net'), may hold values from 0.5 to 1.5
- ctl_in: bfloat16 [4, 3, 3, 4, 320], P('net'), may hold values from -1 to 1
- ctl_hint: bfloat16 [4, 192, 320], P('net'), may hold values from -0.4375 to 0.4375
- ctl_zero0: bfloat16 [4, 320, 320], P('net'), may hold values from -0.3125 to 0.3125
- ctl_gain: bfloat16 [4, 320], P('net'), may hold values from 0.099609375 to 1.8984375
- ctl_conv: bfloat16 [4, 3, 3, 320, 320], P('net'), may hold values from -0.109375 to 0.109375
- ctl_zero1: bfloat16 [4, 320, 320], P('net'), may hold values from -0.3125 to 0.3125
- unet_in: bfloat16 [3, 3, 4, 320], replicated, may hold values from -1 to 1
- unet_gain: bfloat16 [320], replicated, may hold values from 0.099609375 to 1.8984375
- unet_conv: bfloat16 [3, 3, 320, 320], replicated, may hold values from -0.109375 to 0.109375
Outputs:
- skip0: bfloat16 [32, 64, 64, 320], P('net', 'rep')
- skip1: bfloat16 [32, 64, 64, 320], P('net', 'rep')
Inputs may be any that keep to these rules, and one draw needn't show every extreme that they name: `cond_ids`: in each aligned block of 8 requests (those of one index of net) no id is named by more than 4 requests.
All inputs are finite; a program needn't handle non-finite values. No bound on the sum of `valid` on one device may be relied on, other than what follows from the above.
Results may differ from a plain program's by a relative error of at most 0.008.
Values may be sent and summed in bfloat16 or wider, within the bound.
No kernel may reach another device: no remote copies, remote signals or barrier semaphores. Data moves between devices by JAX's collectives and lax.ppermute only.
A program may use at most 256 MiB of HBM per device.

v0:
```python
import jax
import jax.numpy as jnp
from jax import lax
from jax.sharding import PartitionSpec as P

LCH = 4
GROUPS = 32


epsilon = 1e-05


def padded_2(block, sides, width):
    for axis, dim in sides:
        count = lax.axis_size(axis)
        forward = [(i, i + 1) for i in range(count - 1)]
        backward = [(target, source) for source, target in forward]
        low = lax.ppermute(
            lax.slice_in_dim(block, block.shape[dim] - width, None, axis=dim), axis, forward
        )
        high = lax.ppermute(lax.slice_in_dim(block, 0, width, axis=dim), axis, backward)
        block = jnp.concatenate([low, block, high], axis=dim)
    return block


def conv_rows(padded, weight):
    row_count = padded.shape[-3] - 2
    col_count = padded.shape[-2]
    padding = [(0, 0)] * (padded.ndim - 2) + [(1, 1), (0, 0)]
    padded_cols = jnp.pad(padded, padding)
    result = None
    for shift_y in range(3):
        for shift_x in range(3):
            window = padded_cols[
                ..., shift_y : shift_y + row_count, shift_x : shift_x + col_count, :
            ]
            if weight.ndim == 5:
                contribution = jnp.einsum(
                    "brwc,bco->brwo",
                    window,
                    weight[:, shift_y, shift_x],
                    preferred_element_type=jnp.float32,
                )
            else:
                contribution = jnp.dot(
                    window.reshape(-1, window.shape[-1]),
                    weight[shift_y, shift_x],
                    preferred_element_type=jnp.float32,
                )
                contribution = contribution.reshape(window.shape[:-1] + (weight.shape[-1],))
            result = contribution if result is None else result + contribution
    return result


def project(values, weight):
    return jnp.einsum("brwk,bko->brwo", values, weight, preferred_element_type=jnp.float32)


def norm_silu(values, gain, reducer, spread):
    floats = values.astype(jnp.float32)
    first_sums, second_sums = reducer(
        (jnp.sum(floats, axis=(-3, -2)), jnp.sum(floats * floats, axis=(-3, -2)))
    )
    group_size = values.shape[-1] // GROUPS
    count = values.shape[-3] * spread * values.shape[-2] * group_size
    group_mean = first_sums.reshape(first_sums.shape[:-1] + (GROUPS, group_size)).sum(-1) / count
    group_square = (
        second_sums.reshape(second_sums.shape[:-1] + (GROUPS, group_size)).sum(-1) / count
    )
    inverse = lax.rsqrt(group_square - group_mean * group_mean + epsilon)
    mean_chan = jnp.repeat(group_mean, group_size, axis=-1)
    scale_chan = jnp.repeat(inverse, group_size, axis=-1) * gain.astype(jnp.float32)
    normed = (floats - mean_chan[..., None, None, :]) * scale_chan[..., None, None, :]
    return jax.nn.silu(normed).astype(jnp.bfloat16)


def control(lat_padded, hint_grid, weights, rim_fn, reducer, spread):
    weight_in, weight_hint, weight_zero0, weight_gain, weight_conv, weight_zero1 = weights
    first_ctl = (conv_rows(lat_padded, weight_in) + project(hint_grid, weight_hint)).astype(
        jnp.bfloat16
    )
    first_res = project(first_ctl, weight_zero0).astype(jnp.bfloat16)
    ctl_normed = norm_silu(first_ctl, weight_gain, reducer, spread)
    second_ctl = (
        first_ctl.astype(jnp.float32) + conv_rows(rim_fn(ctl_normed), weight_conv)
    ).astype(jnp.bfloat16)
    second_res = project(second_ctl, weight_zero1).astype(jnp.bfloat16)
    return (first_res, second_res)


def shards(
    latent,
    hint,
    cond_ids,
    valid,
    cond_scale,
    ctl_in,
    ctl_hint,
    ctl_zero0,
    ctl_gain,
    ctl_conv,
    ctl_zero1,
    unet_in,
    unet_gain,
    unet_conv,
):
    batch_size, row_count, flat_width = latent.shape
    col_count = flat_width // LCH
    rep_count = lax.axis_size("rep")
    cond_idx = cond_ids[:, 0]
    lat_grid = latent.reshape(batch_size, row_count, col_count, LCH)
    lat_padded = padded_2(lat_grid, (("rep", 1),), 1)
    weighting = (cond_scale * valid.astype(jnp.float32))[:, None, None, None]
    gathered = (
        lax.all_gather(ctl_in, "net", axis=0, tiled=True),
        lax.all_gather(ctl_hint, "net", axis=0, tiled=True),
        lax.all_gather(ctl_zero0, "net", axis=0, tiled=True),
        lax.all_gather(ctl_gain, "net", axis=0, tiled=True),
        lax.all_gather(ctl_conv, "net", axis=0, tiled=True),
        lax.all_gather(ctl_zero1, "net", axis=0, tiled=True),
    )
    weights = tuple((jnp.take(stacked, cond_idx, axis=0) for stacked in gathered))

    def control_rim(values):
        return padded_2(values, (("rep", 1),), 1)

    def control_sums(totals):
        return lax.psum((totals[0], totals[1]), "rep")

    first_res, second_res = control(lat_padded, hint, weights, control_rim, control_sums, rep_count)
    first_float = first_res.astype(jnp.float32)
    second_float = second_res.astype(jnp.float32)

    def unet_sums(totals):
        return lax.psum((totals[0], totals[1]), "rep")

    unet_first = conv_rows(lat_padded, unet_in).astype(jnp.bfloat16)
    unet_normed = norm_silu(unet_first, unet_gain, unet_sums, rep_count)
    normed_padded = padded_2(unet_normed, (("rep", 1),), 1)
    first_skip = (unet_first.astype(jnp.float32) + weighting * first_float).astype(jnp.bfloat16)
    second_skip = (
        unet_first.astype(jnp.float32)
        + conv_rows(normed_padded, unet_conv)
        + weighting * second_float
    ).astype(jnp.bfloat16)
    return (first_skip, second_skip)


def solution(mesh):
    return jax.shard_map(
        shards,
        mesh=mesh,
        in_specs=(
            P("net", "rep", None),
            P("net", "rep", None, None),
            P("net", None),
            P("net"),
            P("net"),
            P("net", None, None, None, None),
            P("net", None, None),
            P("net", None, None),
            P("net", None),
            P("net", None, None, None, None),
            P("net", None, None),
            P(),
            P(),
            P(),
        ),
        out_specs=(P("net", "rep", None, None), P("net", "rep", None, None)),
        check_vma=False,
    )
```

profile of v0, /device:TPU:0, one launch (start us, length us, event | category | flops | bytes accessed | tf_op | source)
XLA Modules:
  0.0 452.1 jit_solution(10847032195741060201)
XLA Ops:
  9.1 4.9 %collective-permute-start = (bf16[8,1,64,4]{2,3,1,0:T(4,128)(2,1)S(1)}, bf16[8,1,64,4]{2,3,1,0:T(4,128)(2,1)S(1)}, u32[]{:S(2)}, u32[]{:S(2)}) collective-permute-start(bf16[8,1,64,4]{2,3,1,0:T(4,128)(2,1)S(1)} %get-tuple-element.15), channel_id=1, source_target_pairs={{0,1},{1,2},{2,3},{3,4},{4,5},{5,6},{6,7},{8,9},{9,10},{10,11},{11... | collective-permute-start | bytes 12296 | tf_op jit(solution)/shard_map/ppermute | solution.py:18
  18.0 5.6 %all_gather.18 = bf16[4,3,3,4,320]{4,3,2,1,0:T(4,128)(2,1)S(1)} all-gather(bf16[1,3,3,4,320]{4,3,2,1,0:T(4,128)(2,1)} %param.21), channel_id=1, replica_groups=mesh['net'=4,'rep'=8] {'net'}, dimensions={0}, use_global_device_ids=true | all-gather | bytes 115200 | tf_op jit(solution)/shard_map/all_gather | solution.py:115
  28.7 11.4 %all_gather.19 = bf16[4,192,320]{2,1,0:T(8,128)(2,1)S(1)} all-gather(bf16[1,192,320]{2,1,0:T(8,128)(2,1)S(1)} %copy-done.11), channel_id=1, replica_groups=mesh['net'=4,'rep'=8] {'net'}, dimensions={0}, use_global_device_ids=true | all-gather | bytes 614400 | tf_op jit(solution)/shard_map/all_gather | solution.py:116
  45.6 16.1 %all_gather.23 = bf16[4,320,320]{2,1,0:T(8,128)(2,1)} all-gather(bf16[1,320,320]{2,1,0:T(8,128)(2,1)S(1)} %copy-done.10), channel_id=1, replica_groups=mesh['net'=4,'rep'=8] {'net'}, dimensions={0}, use_global_device_ids=true | all-gather | bytes 1024000 | tf_op jit(solution)/shard_map/all_gather | solution.py:120
  61.6 15.7 %all_gather.20 = bf16[4,320,320]{2,1,0:T(8,128)(2,1)S(1)} all-gather(bf16[1,320,320]{2,1,0:T(8,128)(2,1)} %param.23), channel_id=1, replica_groups=mesh['net'=4,'rep'=8] {'net'}, dimensions={0}, use_global_device_ids=true | all-gather | bytes 1024000 | tf_op jit(solution)/shard_map/all_gather | solution.py:117
  81.3 5.8 %all-gather = bf16[4,1,320]{2,1,0:T(2,128)(2,1)S(1)} all-gather(bf16[1,1,320]{2,1,0:T(2,128)(2,1)S(1)} %bitcast.316), channel_id=1, replica_groups=mesh['net'=4,'rep'=8] {'net'}, dimensions={0}, use_global_device_ids=true | all-gather | bytes 3200 | tf_op jit(solution)/shard_map/all_gather | solution.py:118
  138.6 19.3 %convert_reduce_fusion.1 = (f32[8,320]{1,0:T(8,128)S(1)}, f32[8,320]{1,0:T(8,128)S(1)}, bf16[8,8,64,320]{3,2,1,0:T(8,128)(2,1)}) fusion(f32[8,320,8,64]{1,3,2,0:T(8,128)} %fusion.82, bf16[8,3,3,4,320]{4,3,0,2,1:T(4,128)(2,1)S(1)} %copy_select_fusion, bf16[8,10,66,4]{2,3,1,0:T(4,128)(2,1)S(1)} %select_maximum_fusion.4, f32[8,8,64,320]{3,2,1,0:T(8,128)} %fusion.137, ...), kind=kOutput, calls=%fused_computation.18 | convolution fusion | flops 28830720 | bytes 50966528 | tf_op jit(solution)/shard_map/brwc,bco->brwo/dot_general | solution.py:38
  165.5 18.7 %convert_reduce_fusion = (f32[8,320]{1,0:T(8,128)S(1)}, f32[8,320]{1,0:T(8,128)S(1)}, bf16[8,8,64,320]{3,2,1,0:T(8,128)(2,1)}) fusion(bf16[3,3,4,320]{3,2,1,0:T(4,128)(2,1)S(1)} %copy-done.13, bf16[8,10,66,4]{2,3,1,0:T(4,128)(2,1)S(1)} %select_maximum_fusion.4, f32[8,8,64,320]{3,2,1,0:T(8,128)} %fusion.140, f32[8,8,64,320]{3,2,1,0:T(8,128)} %fusion.119, ...), kind=kOutput, calls=%fused_computation.13 | convolution fusion | flops 27520000 | bytes 44653568 | tf_op jit(solution)/shard_map/dot_general | solution.py:45
  184.6 45.3 %all-reduce.3 = (f32[8,32,10]{2,1,0:T(8,128)}, f32[8,32,10]{2,1,0:T(8,128)}, f32[8,32,10]{2,1,0:T(8,128)S(1)}, f32[8,32,10]{2,1,0:T(8,128)S(1)}) all-reduce(f32[8,32,10]{2,1,0:T(8,128)S(1)} %reshape.149, f32[8,32,10]{2,1,0:T(8,128)S(1)} %reshape.148, f32[8,32,10]{2,1,0:T(8,128)S(1)} %reshape.152, ...), channel_id=1, replica_groups=mesh['net'=4,'rep'=8] {'rep'}, use_global_device_ids=true, to_apply=%region_4.6 | all-reduce | flops 10240 | bytes 81920 | tf_op jit(solution)/shard_map/psum | solution.py:135
  250.5 6.7 %fusion.10 = bf16[8,8,64,320]{3,2,1,0:T(8,128)(2,1)} fusion(bf16[8,8,64,320]{3,2,1,0:T(8,128)(2,1)} %get-tuple-element.21, f32[8]{0:T(128)S(1)} %convert_multiply_fusion.3, bf16[8,8,64,320]{3,2,1,0:T(8,128)(2,1)} %get-tuple-element.22, bf16[8,320,320]{2,1,0:T(8,128)(2,1)S(1)} %gather_fusion.5, pred[8]{0:T(512)(128)(4,1)S(1)} %compare_and_fusion), kind=kOutput, calls=%fused_computation.29 | convolution fusion | flops 847544320 | bytes 9502760 | tf_op jit(solution)/shard_map/brwk,bko->brwo/dot_general | solution.py:56
  257.2 4.8 %fusion.93 = f32[8,8,64,320]{3,2,1,0:T(8,128)} fusion(bf16[8,8,64,320]{3,2,1,0:T(8,128)(2,1)S(1)} %fusion.17, bf16[3,3,320,320]{3,2,1,0:T(8,128)(2,1)S(1)} %copy-done.9), kind=kOutput, calls=%fused_computation.123 | convolution fusion | flops 838860800 | bytes 8634368 | tf_op jit(solution)/shard_map/dot_general | solution.py:45
  273.2 4.8 %fusion.59 = f32[8,8,64,320]{3,2,1,0:T(8,128)} fusion(bf16[8,10,66,320]{3,2,1,0:T(8,128)(2,1)S(1)} %select_maximum_fusion.2, bf16[3,3,320,320]{3,2,1,0:T(8,128)(2,1)S(1)} %copy-done.9), kind=kOutput, calls=%fused_computation.84 | convolution fusion | flops 838860800 | bytes 8634368 | tf_op jit(solution)/shard_map/dot_general | solution.py:45
  297.0 4.9 %fusion.31 = f32[8,8,64,320]{3,2,1,0:T(8,128)} fusion(bf16[8,1,64,320]{3,2,1,0:T(8,128)(2,1)S(1)} %collective-permute-done.3, bf16[8,8,64,320]{3,2,1,0:T(8,128)(2,1)S(1)} %fusion.17, bf16[3,3,320,320]{3,2,1,0:T(8,128)(2,1)S(1)} %copy-done.9), kind=kOutput, calls=%fused_computation.57 | convolution fusion | flops 844759040 | bytes 9027584 | tf_op jit(solution)/shard_map/dot_general | solution.py:45
  305.6 7.1 %mini-gather-slice.2 = bf16[4,3,3,256,320]{4,3,2,1,0:T(8,128)(2,1)} slice(bf16[4,3,3,320,320]{4,3,2,1,0:T(8,128)(2,1)} %all-gather.3.cloned.1.call-done), slice={[0:4], [0:3], [0:3], [0:256], [0:320]} | slice | bytes 11796480 | tf_op jit(solution)/shard_map/jit(_take)/gather | solution.py:122
  312.6 9.4 %copy.86 = bf16[4,3,3,256,320]{3,4,2,1,0:T(8,128)(2,1)} copy(bf16[4,3,3,256,320]{4,3,2,1,0:T(8,128)(2,1)} %mini-gather-slice.2) | data formatting | bytes 11796480
  322.0 8.8 %gather_fusion.3 = bf16[8,3,3,256,320]{3,4,2,1,0:T(8,128)(2,1)} fusion(bf16[4,3,3,256,320]{3,4,2,1,0:T(8,128)(2,1)} %copy.86, s32[1024]{0:T(1024)S(1)} %pad_clamp_fusion.1), kind=kCustom, calls=%fused_computation.5 | custom fusion | bytes 23592992 | tf_op jit(solution)/shard_map/jit(_take)/gather | solution.py:122
  330.8 17.1 %copy.44 = bf16[8,3,3,256,320]{4,3,0,2,1:T(8,128)(2,1)} copy(bf16[8,3,3,256,320]{3,4,2,1,0:T(8,128)(2,1)} %gather_fusion.3) | data formatting | bytes 23592960 | tf_op jit(solution)/shard_map/jit(_take)/gather | solution.py:122
  350.6 11.1 %maximum_select_fusion = bf16[8,3,3,320,320]{4,3,0,2,1:T(8,128)(2,1)S(1)} fusion(bf16[8,3,3,256,320]{4,3,0,2,1:T(8,128)(2,1)} %copy.44, pred[8]{0:T(512)(128)(4,1)S(1)} %and_bitcast_fusion, bf16[8,3,3,64,320]{4,3,2,1,0:T(8,128)(2,1)} %gather_fusion.4), kind=kLoop, calls=%fused_computation.7 | loop fusion | flops 36864000 | bytes 29491208 | tf_op jit(solution)/shard_map/jit(_take)/select_n | solution.py:122
  361.8 5.3 %fusion.55 = f32[8,8,64,320]{3,2,1,0:T(8,128)} fusion(bf16[8,10,66,320]{3,2,1,0:T(8,128)(2,1)S(1)} %bitcast.311, bf16[8,3,3,320,320]{4,3,0,2,1:T(8,128)(2,1)S(1)} %maximum_select_fusion), kind=kOutput, calls=%fused_computation.80 | convolution fusion | flops 838860800 | bytes 10354688 | tf_op jit(solution)/shard_map/brwc,bco->brwo/dot_general | solution.py:38
  367.1 4.8 %fusion.53 = f32[8,8,64,320]{3,2,1,0:T(8,128)} fusion(bf16[8,10,66,320]{3,2,1,0:T(8,128)(2,1)S(1)} %bitcast.311, bf16[8,3,3,320,320]{4,3,0,2,1:T(8,128)(2,1)S(1)} %maximum_select_fusion), kind=kOutput, calls=%fused_computation.78 | convolution fusion | flops 838860800 | bytes 10354688 | tf_op jit(solution)/shard_map/brwc,bco->brwo/dot_general | solution.py:38
  376.7 4.8 %fusion.49 = f32[8,8,64,320]{3,2,1,0:T(8,128)} fusion(bf16[8,10,66,320]{3,2,1,0:T(8,128)(2,1)S(1)} %bitcast.311, bf16[8,3,3,320,320]{4,3,0,2,1:T(8,128)(2,1)S(1)} %maximum_select_fusion), kind=kOutput, calls=%fused_computation.74 | convolution fusion | flops 838860800 | bytes 10354688 | tf_op jit(solution)/shard_map/brwc,bco->brwo/dot_general | solution.py:38
  386.2 4.9 %fusion.75 = f32[8,8,64,320]{3,2,1,0:T(8,128)} fusion(bf16[8,8,64,320]{3,2,1,0:T(8,128)(2,1)S(1)} %copy-done.6, bf16[8,3,3,320,320]{4,3,0,2,1:T(8,128)(2,1)S(1)} %maximum_select_fusion), kind=kOutput, calls=%fused_computation.99 | convolution fusion | flops 838860800 | bytes 10354688 | tf_op jit(solution)/shard_map/brwc,bco->brwo/dot_general | solution.py:38
  400.6 21.9 %fusion.43 = bf16[8,8,64,320]{3,2,1,0:T(8,128)(2,1)} fusion(bf16[8,8,64,320]{3,2,1,0:T(8,128)(2,1)} %get-tuple-element.22, f32[8,8,64,320]{3,2,1,0:T(8,128)} %fusion.39, f32[8,8,64,320]{3,2,1,0:T(8,128)} %fusion.47, f32[8,8,64,320]{3,2,1,0:T(8,128)} %fusion.49, f32[8,8,64,320]{3,2,1,0:T(8,128)} %fusion.75, f32[8,8,64,320]{3,2,1,0:T(8,128)} %fusion.51, ...), kind=kOutput, calls=%fused_computation.69 | convolution fusion | flops 1692958720 | bytes 62849032 | tf_op jit(solution)/shard_map/brwk,bko->brwo/dot_general | solution.py:56
  422.5 22.5 %fusion.20 = bf16[8,8,64,320]{3,2,1,0:T(8,128)(2,1)} fusion(bf16[8,8,64,320]{3,2,1,0:T(8,128)(2,1)} %get-tuple-element.21, f32[8,8,64,320]{3,2,1,0:T(8,128)} %fusion.31, f32[8,8,64,320]{3,2,1,0:T(8,128)} %fusion.59, f32[8,8,64,320]{3,2,1,0:T(8,128)} %fusion.61, f32[8,8,64,320]{3,2,1,0:T(8,128)} %fusion.93, f32[8,8,64,320]{3,2,1,0:T(8,128)} %fusion.63, ...), kind=kOutput, calls=%fused_computation.39 | convolution fusion | flops 857210880 | bytes 62636064 | tf_op jit(solution)/shard_map/dot_general | solution.py:45
  (134 shorter events, 155.7 us)
Async XLA Ops:
  7.2 70.2 %copy-start = (bf16[8,8,64,192]{3,2,1,0:T(8,128)(2,1)S(1)}, bf16[8,8,64,192]{3,2,1,0:T(8,128)(2,1)}, u32[]{:S(2)}) copy-start(bf16[8,8,64,192]{3,2,1,0:T(8,128)(2,1)} %param.17) | copy-start | bytes 4718596
  7.2 21.5 %copy-start.11 = (bf16[1,192,320]{2,1,0:T(8,128)(2,1)S(1)}, bf16[1,192,320]{2,1,0:T(8,128)(2,1)}, u32[]{:S(2)}) copy-start(bf16[1,192,320]{2,1,0:T(8,128)(2,1)} %param.22) | copy-start | bytes 368644
  7.2 298.4 %all-gather.3.cloned.1.call-start = ((), (), s32[]{:S(2)}) async-start(), calls=%async_computation | async-start | bytes 11059200 | tf_op jit(solution)/shard_map/all_gather | solution.py:119
  9.1 83.0 %collective-permute-start = (bf16[8,1,64,4]{2,3,1,0:T(4,128)(2,1)S(1)}, bf16[8,1,64,4]{2,3,1,0:T(4,128)(2,1)S(1)}, u32[]{:S(2)}, u32[]{:S(2)}) collective-permute-start(bf16[8,1,64,4]{2,3,1,0:T(4,128)(2,1)S(1)} %get-tuple-element.15), channel_id=1, source_target_pairs={{0,1},{1,2},{2,3},{3,4},{4,5},{5,6},{6,7},{8,9},{9,10},{10,11},{11... | collective-permute-start | bytes 12296 | tf_op jit(solution)/shard_map/ppermute | solution.py:18
  14.0 27.8 %copy-start.13 = (bf16[3,3,4,320]{3,2,1,0:T(4,128)(2,1)S(1)}, bf16[3,3,4,320]{3,2,1,0:T(4,128)(2,1)}, u32[]{:S(2)}) copy-start(bf16[3,3,4,320]{3,2,1,0:T(4,128)(2,1)} %param.27) | copy-start | bytes 69124
  14.0 78.0 %collective-permute-start.1 = (bf16[8,1,64,4]{2,3,1,0:T(4,128)(2,1)S(1)}, bf16[8,1,64,4]{2,3,1,0:T(4,128)(2,1)S(1)}, u32[]{:S(2)}, u32[]{:S(2)}) collective-permute-start(bf16[8,1,64,4]{2,3,1,0:T(4,128)(2,1)S(1)} %get-tuple-element.16), channel_id=1, source_target_pairs={{1,0},{2,1},{3,2},{4,3},{5,4},{6,5},{7,6},{9,8},{10,9},{11,10},{12... | collective-permute-start | bytes 12296 | tf_op jit(solution)/shard_map/ppermute | solution.py:21
  28.7 16.8 %copy-start.10 = (bf16[1,320,320]{2,1,0:T(8,128)(2,1)S(1)}, bf16[1,320,320]{2,1,0:T(8,128)(2,1)}, u32[]{:S(2)}) copy-start(bf16[1,320,320]{2,1,0:T(8,128)(2,1)} %param.26) | copy-start | bytes 614404
  41.8 35.5 %copy-start.8 = (bf16[8,192,320]{2,1,0:T(8,128)(2,1)S(1)}, bf16[8,192,320]{2,1,0:T(8,128)(2,1)}, u32[]{:S(2)}) copy-start(bf16[8,192,320]{2,1,0:T(8,128)(2,1)} %gather_fusion.1) | copy-start | bytes 2949124
  45.5 35.8 %copy-start.16 = (f32[8]{0:T(128)S(1)}, f32[8]{0:T(128)}, u32[]{:S(2)}) copy-start(f32[8]{0:T(128)} %param.20) | copy-start | bytes 100
  45.5 35.8 %copy-start.17 = (s32[8]{0:T(128)S(1)}, s32[8]{0:T(128)}, u32[]{:S(2)}) copy-start(s32[8]{0:T(128)} %param.19) | copy-start | bytes 100
  45.5 35.8 %copy-start.14 = (bf16[1,320]{1,0:T(2,128)(2,1)S(1)}, bf16[1,320]{1,0:T(2,128)(2,1)}, u32[]{:S(2)}) copy-start(bf16[1,320]{1,0:T(2,128)(2,1)} %param.24) | copy-start | bytes 1924
  45.5 42.2 %copy-start.15 = (bf16[320]{0:T(512)(128)(2,1)S(1)}, bf16[320]{0:T(512)(128)(2,1)}, u32[]{:S(2)}) copy-start(bf16[320]{0:T(512)(128)(2,1)} %param.28) | copy-start | bytes 1924
  127.2 11.5 %slice-start.2 = ((s8[6291456]{0:T(1024)(128)(4,1)}), s8[4194304]{0:T(1024)(128)(4,1)S(1)}, s32[]{:S(2)}) async-start(s8[6291456]{0:T(1024)(128)(4,1)} %bitcast.312), calls=%async_computation.3 | async-start | bytes 8388608
  230.6 9.6 %copy-start.12 = (f32[8,32,10]{2,1,0:T(8,128)S(1)}, f32[8,32,10]{2,1,0:T(8,128)}, u32[]{:S(2)}) copy-start(f32[8,32,10]{2,1,0:T(8,128)} %get-tuple-element.7) | copy-start | bytes 30724
  236.5 65.4 %collective-permute-start.4 = (bf16[8,1,64,320]{3,2,1,0:T(8,128)(2,1)}, bf16[8,1,64,320]{3,2,1,0:T(8,128)(2,1)S(1)}, u32[]{:S(2)}, u32[]{:S(2)}) collective-permute-start(bf16[8,1,64,320]{3,2,1,0:T(8,128)(2,1)} %get-tuple-element.11), channel_id=1, source_target_pairs={{0,1},{1,2},{2,3},{3,4},{4,5},{5,6},{6,7},{8,9},{9,10},{10,11},{11... | collective-permute-start | bytes 983048 | tf_op jit(solution)/shard_map/ppermute | solution.py:18
  237.8 64.1 %collective-permute-start.5 = (bf16[8,1,64,320]{3,2,1,0:T(8,128)(2,1)S(1)}, bf16[8,1,64,320]{3,2,1,0:T(8,128)(2,1)S(1)}, u32[]{:S(2)}, u32[]{:S(2)}) collective-permute-start(bf16[8,1,64,320]{3,2,1,0:T(8,128)(2,1)S(1)} %get-tuple-element.12), channel_id=1, source_target_pairs={{1,0},{2,1},{3,2},{4,3},{5,4},{6,5},{7,6},{9,8},{10,9},{11,10},{12... | collective-permute-start | bytes 983048 | tf_op jit(solution)/shard_map/ppermute | solution.py:21
  244.2 21.4 %collective-permute-start.2 = (bf16[8,1,64,320]{3,2,1,0:T(8,128)(2,1)S(1)}, bf16[8,1,64,320]{3,2,1,0:T(8,128)(2,1)S(1)}, u32[]{:S(2)}, u32[]{:S(2)}) collective-permute-start(bf16[8,1,64,320]{3,2,1,0:T(8,128)(2,1)S(1)} %get-tuple-element.13), channel_id=1, source_target_pairs={{0,1},{1,2},{2,3},{3,4},{4,5},{5,6},{6,7},{8,9},{9,10},{10,11},{11... | collective-permute-start | bytes 983048 | tf_op jit(solution)/shard_map/ppermute | solution.py:18
  248.8 21.6 %collective-permute-start.3 = (bf16[8,1,64,320]{3,2,1,0:T(8,128)(2,1)S(1)}, bf16[8,1,64,320]{3,2,1,0:T(8,128)(2,1)S(1)}, u32[]{:S(2)}, u32[]{:S(2)}) collective-permute-start(bf16[8,1,64,320]{3,2,1,0:T(8,128)(2,1)S(1)} %get-tuple-element.14), channel_id=1, source_target_pairs={{1,0},{2,1},{3,2},{4,3},{5,4},{6,5},{7,6},{9,8},{10,9},{11,10},{12... | collective-permute-start | bytes 983048 | tf_op jit(solution)/shard_map/ppermute | solution.py:21
  273.2 19.0 %copy-start.2 = (bf16[8,10,66,320]{3,2,1,0:T(8,128)(2,1)}, bf16[8,10,66,320]{3,2,1,0:T(8,128)(2,1)S(1)}, u32[]{:S(2)}) copy-start(bf16[8,10,66,320]{3,2,1,0:T(8,128)(2,1)S(1)} %select_maximum_fusion.2) | copy-start | bytes 10137604
  330.8 17.1 %slice-start.4 = ((bf16[4,3,3,320,320]{4,3,2,1,0:T(8,128)(2,1)}), bf16[4,3,3,64,320]{4,3,2,1,0:T(8,128)(2,1)S(1)}, s32[]{:S(2)}) async-start(bf16[4,3,3,320,320]{4,3,2,1,0:T(8,128)(2,1)} %all-gather.3.cloned.1.call-done), calls=%async_computation.5 | async-start | bytes 3538944 | tf_op jit(solution)/shard_map/jit(_take)/gather | solution.py:122
  347.9 13.9 %slice-start = ((s8[4423680]{0:T(1024)(128)(4,1)}), s8[229376]{0:T(1024)(128)(4,1)S(1)}, s32[]{:S(2)}) async-start(s8[4423680]{0:T(1024)(128)(4,1)} %bitcast.310), calls=%async_computation.1 | async-start | bytes 458752
  350.6 11.1 %slice-start.1 = ((s8[4423680]{0:T(1024)(128)(4,1)}), s8[4194304]{0:T(1024)(128)(4,1)S(1)}, s32[]{:S(2)}) async-start(s8[4423680]{0:T(1024)(128)(4,1)} %bitcast.310), calls=%async_computation.2 | async-start | bytes 8388608
  361.8 34.0 %copy-start.3 = (bf16[8,3,3,320,320]{4,3,0,2,1:T(8,128)(2,1)}, bf16[8,3,3,320,320]{4,3,0,2,1:T(8,128)(2,1)S(1)}, u32[]{:S(2)}) copy-start(bf16[8,3,3,320,320]{4,3,0,2,1:T(8,128)(2,1)S(1)} %maximum_select_fusion) | copy-start | bytes 44236804
  422.5 22.5 %copy-start.1 = (bf16[8,8,64,192]{3,2,1,0:T(8,128)(2,1)S(1)}, bf16[8,8,64,192]{3,2,1,0:T(8,128)(2,1)}, u32[]{:S(2)}) copy-start(bf16[8,8,64,192]{3,2,1,0:T(8,128)(2,1)} %param.17) | copy-start | bytes 4718596
  (6 other events, 32.0 us)
Sparse Core Ops, SparseCore 0:
  15.4 76.9 all-gather.2
where the time goes:
time: 458 us; the launch traced here: 452 us
  matrix products  232 us (51%)
  blocking collectives  99.9 us (22%)
  local copies, waits for them, and re-layouts  58.2 us (13%)
  other arithmetic  28.8 us (6%)
  starting transfers between devices  15 us (3%)
  between operations  14.7 us (3%)
    dot_general x18, matrix products, conv_rows(): jnp.dot(window.reshape(-1, window.shape[-1]), weight[shift_y, shift_x], p...  110 us
    dot_general x17, matrix products, conv_rows(): jnp.einsum('brwc,bco->brwo', window, weight[:, shift_y, shift_x], preferr...  89.7 us
    psum x1, blocking collectives, unet_sums(): return lax.psum((totals[0], totals[1]), 'rep')  45.3 us
    gather x11, local copies, waits for them, and re-layouts, shards(): jnp.take(stacked, cond_idx, axis=0)  43 us
    dot_general x3, matrix products, project(): jnp.einsum('brwk,bko->brwo', values, weight, preferred_element_type=jnp.f...  32.5 us
    all_gather x1, blocking collectives, shards(): lax.all_gather(ctl_zero1, 'net', axis=0, tiled=True)  16.1 us
    all_gather x1, blocking collectives, shards(): lax.all_gather(ctl_zero0, 'net', axis=0, tiled=True)  15.7 us
    select_n x4, other arithmetic, shards(): jnp.take(stacked, cond_idx, axis=0)  12.6 us
  transfers between devices with their start and end apart: 7, of which 1 were waited for; matrix products, arithmetic and copies ran while one was open for 39% of the time, Pallas kernels for 0%

commit v1 on v0

v1 whole, which is shorter than its diff:
```python
import functools

import jax
import jax.numpy as jnp
from jax import lax
from jax.experimental import pallas as pl
from jax.experimental.pallas import tpu as pltpu
from jax.sharding import PartitionSpec as P


LCH = 4
GROUPS = 32
LANES = 128
EPS = 1e-05
CHUNKS = 3


def up_to(value, step):
    return -(-value // step) * step


def cost(flops):
    return pl.CostEstimate(flops=flops, transcendentals=0, bytes_accessed=1 << 20)


def params(mib):
    return pltpu.CompilerParams(
        dimension_semantics=("arbitrary",), vmem_limit_bytes=mib * 1024 * 1024
    )


def main_of(channels):
    return channels // 256 * 256


def slot_of(cond, nets):
    at = lax.axis_index("net")
    return 2 * lax.rem((at >> 1) - (cond >> 1) + nets // 2, nets // 2) + ((at ^ cond) & 1)


def fill_stem(target, hint_weight, in_weight):
    width = hint_weight.shape[0]
    target[0:width, :] = hint_weight.astype(jnp.float32)
    target[width:, :] = jnp.zeros((target.shape[0] - width, target.shape[1]), jnp.float32)
    for dy in range(3):
        for dx in range(3):
            low = width + (3 * dy + dx) * LCH
            target[low : low + LCH, :] = in_weight[dy, dx].astype(jnp.float32)


def compose_kernel(*refs):
    sources, outs = refs[:5], refs[5 : 5 + 2 * CHUNKS]
    conv_ref, hint_ref, in_ref, zero0_ref, zero1_ref, stem, both, whole_half, sems = refs[
        5 + 2 * CHUNKS :
    ]
    copies = [
        pltpu.make_async_copy(src.at[0], dst, sems.at[i])
        for i, (src, dst) in enumerate(
            zip(sources, (conv_ref, hint_ref, in_ref, zero0_ref, zero1_ref))
        )
    ]
    for copy in copies[::-1]:
        copy.start()
    both[...] = jnp.zeros_like(both)
    chans = conv_ref.shape[2]
    part = chans // 2
    main = main_of(chans)
    lanes = up_to(chans, LANES)
    for copy in copies[1:]:
        copy.wait()
    fill_stem(stem, hint_ref[...], in_ref[...])
    both[:, 0:chans] = zero0_ref[...]
    both[:, lanes : lanes + chans] = zero1_ref[...]
    copies[0].wait()
    second_main = both[:, lanes : lanes + main]
    second_tail = both[:, lanes + main : 2 * lanes]
    stem_part = stem.shape[0] // 2
    for order in range(2):
        half = (lax.axis_index("rep") & 1) ^ order
        lhs = stem[pl.ds(half * stem_part, stem_part), :].astype(jnp.bfloat16)
        heads = jnp.dot(lhs, both[...], preferred_element_type=jnp.float32)
        whole_half[0:stem_part, :] = heads.astype(jnp.bfloat16)

        def put(at, width, values):
            whole_half[stem_part:, at : at + width] = values.astype(jnp.bfloat16)

        tails = []
        for dx in range(3):
            lhs = conv_ref[:, dx, pl.ds(half * part, part), :].reshape(3 * part, chans)
            put(dx * main, main, jnp.dot(lhs, second_main, preferred_element_type=jnp.float32))
            tails.append(jnp.dot(lhs, second_tail, preferred_element_type=jnp.float32))
        put(3 * main, LANES, tails[0] + pltpu.roll(tails[1], LANES // 2, 1))
        put(3 * main + LANES, LANES, tails[2])
        low = 0
        for out in outs[CHUNKS * order : CHUNKS * (order + 1)]:
            out[...] = whole_half[low : low + out.shape[0], :]
            low += out.shape[0]


def chunk_rows(rows):
    step = up_to(rows // CHUNKS, 16)
    return [step] * (CHUNKS - 1) + [rows - step * (CHUNKS - 1)]


def compose(ctl_conv, ctl_hint, ctl_in, ctl_zero0, ctl_zero1, depth):
    chans = ctl_conv.shape[3]
    wide = 3 * main_of(chans) + 2 * LANES
    rows = depth // 2 + 3 * (chans // 2)
    shapes = [(size, wide) for size in chunk_rows(rows)] * 2
    sources = (ctl_conv, ctl_hint, ctl_in, ctl_zero0, ctl_zero1)
    return pl.pallas_call(
        compose_kernel,
        in_specs=[pl.BlockSpec(memory_space=pltpu.HBM)] * len(sources),
        out_shape=[jax.ShapeDtypeStruct(shape, jnp.bfloat16) for shape in shapes],
        scratch_shapes=[pltpu.VMEM(array.shape[1:], jnp.bfloat16) for array in sources]
        + [
            pltpu.VMEM((depth, chans), jnp.float32),
            pltpu.VMEM((chans, wide), jnp.bfloat16),
            pltpu.VMEM((rows, wide), jnp.bfloat16),
            pltpu.SemaphoreType.DMA((len(sources),)),
        ],
        compiler_params=pltpu.CompilerParams(vmem_limit_bytes=20 * 1024 * 1024),
        cost_estimate=cost(2 * 1216 * 320 * 1024 * 2),
        name="compose",
    )(*sources)


def arrange_kernel(conv_ref, out_ref):
    chans = conv_ref.shape[2]
    main = main_of(chans)
    tail = chans - main
    row = lax.broadcasted_iota(jnp.int32, (chans, LANES), 0)
    col = lax.broadcasted_iota(jnp.int32, (chans, LANES), 1)
    pick = jnp.where(row == col + main, 1.0, 0.0).astype(jnp.bfloat16)
    for dy in range(3):
        tails = []

        def put(at, values):
            width = values.shape[1]
            out_ref[dy * main : (dy + 1) * main, at : at + width] = values[0:main]
            low = 3 * main + dy * tail
            out_ref[low : low + tail, at : at + width] = values[main:]

        for dx in range(3):
            put(dx * main, conv_ref[dy, dx, :, 0:main])
            tails.append(jnp.dot(conv_ref[dy, dx], pick, preferred_element_type=jnp.float32))
        put(3 * main, (tails[0] + pltpu.roll(tails[1], LANES // 2, 1)).astype(jnp.bfloat16))
        put(3 * main + LANES, tails[2].astype(jnp.bfloat16))
    out_ref[3 * chans :, :] = jnp.zeros(
        (out_ref.shape[0] - 3 * chans, out_ref.shape[1]), jnp.bfloat16
    )


def arrange(unet_conv):
    wide = 3 * main_of(unet_conv.shape[2]) + 2 * LANES
    return pl.pallas_call(
        arrange_kernel,
        out_shape=jax.ShapeDtypeStruct((wide, wide), jnp.bfloat16),
        compiler_params=pltpu.CompilerParams(vmem_limit_bytes=12 * 1024 * 1024),
        cost_estimate=cost(2 * 2880 * 320 * 256),
        name="arrange",
    )(unet_conv)


def stem_kernel(
    cond_ref, lat_ref, hint_ref, top_ref, bot_ref, unet_ref, *rest,
    nets,
):
    stems = rest[: 3 * nets]
    (
        u_ref, h_ref, a_ref, sums_ref, gain_ref,
        weights, grid_in, lone, spread_rows, pick, gains,
    ) = rest[3 * nets :]
    step = pl.program_id(0)
    _, _, double = weights.shape
    half = double // 2
    chans = unet_ref.shape[3]
    _, rows, cols, width = hint_ref.shape
    flat = lat_ref.shape[2]
    bits = LCH.bit_length() - 1

    @pl.when(step == 0)
    def _():
        gains[...] = jnp.zeros_like(gains)
        weights[...] = jnp.zeros_like(weights)
        fill_stem(lone, jnp.zeros((width, chans), jnp.bfloat16), unet_ref[...])
        for n in range(nets):
            weights[n, :, 0:chans] = lone[...].astype(jnp.bfloat16)
        for n in range(nets):
            fill_stem(lone, stems[3 * n + 2][0], stems[3 * n][0])
            weights[n, :, half : half + chans] = lone[...].astype(jnp.bfloat16)
            gains[n : n + 1, 0:chans] = stems[3 * n + 1][...].astype(jnp.float32)
        row = lax.broadcasted_iota(jnp.int32, (flat, LANES), 0)
        col = lax.broadcasted_iota(jnp.int32, (flat, LANES), 1) - width % LANES
        chosen = ((row & (LCH - 1)) == (col & (LCH - 1))) & (col >= 0) & (col < 9 * LCH)
        pick[...] = jnp.where(chosen, 1.0, 0.0).astype(jnp.bfloat16)

    at_x = lax.broadcasted_iota(jnp.int32, (cols, flat), 0)
    of_x = lax.broadcasted_iota(jnp.int32, (cols, flat), 1) >> bits
    lat_rows = (
        [(top_ref, cols + r) for r in range(2)]
        + [(lat_ref, r) for r in range(rows)]
        + [(bot_ref, cols + r) for r in range(2)]
    )
    for i, (ref, r) in enumerate(lat_rows):
        line = ref[0, r : r + 1, :].astype(jnp.float32)
        spread_rows[i * cols : (i + 1) * cols, :] = jnp.where(of_x == at_x, line, 0.0).astype(
            jnp.bfloat16
        )
    cells = jnp.dot(spread_rows[...], pick[...], preferred_element_type=jnp.float32)
    total = (rows + 2) * cols
    size = cells.shape[0]
    tap = (lax.broadcasted_iota(jnp.int32, (1, LANES), 1) - width % LANES) >> bits
    tap_y = (tap >= 3).astype(jnp.int32) + (tap >= 6).astype(jnp.int32)
    tap_x = tap - 3 * tap_y
    place = lax.broadcasted_iota(jnp.int32, (size, 1), 0) & (cols - 1)
    left = jnp.where(place != 0, pltpu.roll(cells, 1, 0), 0.0)
    right = jnp.where(place != cols - 1, pltpu.roll(cells, size - 1, 0), 0.0)
    beside = jnp.where(tap_x == 0, left, jnp.where(tap_x == 1, cells, right))
    patches = jnp.where(
        tap_y == 0,
        beside[0:total],
        jnp.where(tap_y == 1, beside[cols : cols + total], beside[2 * cols :]),
    ).astype(jnp.bfloat16)

    grid_in[0:cols, 0:width] = top_ref[0, 0:cols, 0:width]
    grid_in[cols : total - cols, 0:width] = hint_ref[0].reshape(rows * cols, width)
    grid_in[total - cols : total, 0:width] = bot_ref[0, 0:cols, 0:width]
    grid_in[:, width:] = patches[:, width % LANES :]
    a_ref[0] = grid_in[cols : total - cols, :]
    slot = slot_of(cond_ref[step, 0], nets)
    out = jnp.dot(grid_in[...], weights[slot], preferred_element_type=jnp.float32).astype(
        jnp.bfloat16
    )
    u_ref[0] = out[:, 0:half].reshape(rows + 2, cols, half)
    h_ref[0] = out[:, half:].reshape(rows + 2, cols, half)
    own = out[cols : total - cols].astype(jnp.float32)
    first = jnp.sum(own, axis=0, keepdims=True)
    second = jnp.sum(own * own, axis=0, keepdims=True)
    sums_ref[0] = jnp.concatenate(
        [first[:, 0:half], second[:, 0:half], first[:, half:], second[:, half:]], axis=0
    )
    gain_ref[0] = gains[pl.ds(slot, 1), :]


def whole(array, space=None):
    zeros = (0,) * array.ndim
    if space is not None:
        return pl.BlockSpec(memory_space=space)
    return pl.BlockSpec(array.shape, lambda b: zeros)


def per_request(array):
    rest = (0,) * (array.ndim - 1)
    return pl.BlockSpec((1,) + tuple(array.shape[1:]), lambda b: (b,) + rest)


def stem_call(cond_ids, latent, hint, top, bot, unet_in, stems, depth):
    batch, rows, cols, _ = hint.shape
    nets = len(stems) // 3
    chans = unet_in.shape[3]
    half = up_to(chans, LANES)
    total = (rows + 2) * cols
    flat = latent.shape[2]
    outs = [
        jax.ShapeDtypeStruct((batch, rows + 2, cols, half), jnp.bfloat16),
        jax.ShapeDtypeStruct((batch, rows + 2, cols, half), jnp.bfloat16),
        jax.ShapeDtypeStruct((batch, rows * cols, depth), jnp.bfloat16),
        jax.ShapeDtypeStruct((batch, 4, half), jnp.float32),
        jax.ShapeDtypeStruct((batch, 1, half), jnp.float32),
    ]
    blocked = [latent, hint, top, bot]
    return pl.pallas_call(
        functools.partial(stem_kernel, nets=nets),
        grid=(batch,),
        in_specs=[whole(cond_ids, pltpu.SMEM)]
        + [per_request(array) for array in blocked]
        + [whole(unet_in)]
        + [whole(array) for array in stems],
        out_specs=[per_request(array) for array in outs],
        out_shape=outs,
        scratch_shapes=[
            pltpu.VMEM((nets, depth, 2 * half), jnp.bfloat16),
            pltpu.VMEM((total, depth), jnp.bfloat16),
            pltpu.VMEM((depth, chans), jnp.float32),
            pltpu.VMEM(((rows + 4) * cols, flat), jnp.bfloat16),
            pltpu.VMEM((flat, LANES), jnp.bfloat16),
            pltpu.VMEM((up_to(nets, 8), half), jnp.float32),
        ],
        compiler_params=params(14),
        cost_estimate=cost(2 * batch * total * 256 * 896),
        name="stem",
    )(cond_ids, *blocked, unet_in, *stems)


def group_affine(sums_ref, more_ref, which, gain, count, group, chans, scale_ref, shift_ref):
    lanes = sums_ref.shape[2]
    first = sums_ref[:, 2 * which, :] + more_ref[:, 2 * which, :]
    second = sums_ref[:, 2 * which + 1, :] + more_ref[:, 2 * which + 1, :]
    row = lax.broadcasted_iota(jnp.int32, (lanes, lanes), 0)
    col = lax.broadcasted_iota(jnp.int32, (lanes, lanes), 1)
    row_group = jnp.floor((row.astype(jnp.float32) + 0.5) * (1.0 / group))
    col_group = jnp.floor((col.astype(jnp.float32) + 0.5) * (1.0 / group))
    same = jnp.where((row_group == col_group) & (row < chans), 1.0, 0.0)
    mean = jnp.dot(first, same, precision=lax.Precision.HIGHEST) * (1.0 / count)
    square = jnp.dot(second, same, precision=lax.Precision.HIGHEST) * (1.0 / count)
    scale = lax.rsqrt(square - mean * mean + EPS) * gain
    scale_ref[...] = scale
    shift_ref[...] = -mean * scale


def normed_columns(values, scale, shift, lhs, rows, cols):
    normed = values.astype(jnp.float32) * (0.5 * scale) + 0.5 * shift
    normed = normed + normed * jnp.tanh(normed)
    total = (rows + 2) * cols
    main = main_of(values.shape[1])
    at = lax.axis_index("rep")
    last = lax.axis_size("rep") - 1
    place = lax.broadcasted_iota(jnp.int32, (total, 1), 0)
    keep = ((place >= cols) | (at != 0)) & ((place < total - cols) | (at != last))
    normed = jnp.where(keep, normed, 0.0)
    top = normed[:, 0:main].astype(jnp.bfloat16)
    rest = normed[:, main:]
    inner = rows * cols
    for dy in range(3):
        lhs[:, dy * main : (dy + 1) * main] = top[dy * cols : dy * cols + inner]
    pair = rest[0:inner] + pltpu.roll(rest[cols : cols + inner], LANES // 2, 1)
    lhs[:, 3 * main : 3 * main + LANES] = pair.astype(jnp.bfloat16)
    lhs[:, 3 * main + LANES :] = rest[2 * cols : 2 * cols + inner].astype(jnp.bfloat16)


def spread(product, cols):
    inner = product.shape[0]
    main = product.shape[1] // 4
    place = lax.broadcasted_iota(jnp.int32, (inner, 1), 0) % cols
    left = place != 0
    right = place != cols - 1

    def after(values):
        return jnp.where(left, pltpu.roll(values, 1, 0), 0.0)

    def before(values):
        return jnp.where(right, pltpu.roll(values, inner - 1, 0), 0.0)

    head = (
        after(product[:, 0:main])
        + product[:, main : 2 * main]
        + before(product[:, 2 * main : 3 * main])
    )
    low = product[:, 3 * main : 3 * main + LANES]
    high = product[:, 3 * main + LANES :]
    tail = after(low) + pltpu.roll(low, LANES // 2, 1) + before(high)
    return jnp.concatenate([head, tail], axis=1)


def unet_kernel(
    sums_ref, more_ref, gain_ref, pair_ref, next_ref, weight_ref, out_ref,
    scale, shift, even, odd, *, count, group, chans,
):
    step = pl.program_id(0)
    batch = sums_ref.shape[0]
    _, total_rows, cols, lanes = pair_ref.shape
    rows = total_rows - 2
    inner = rows * cols

    def make(values, b, target):
        values = values.reshape(total_rows * cols, lanes)
        normed_columns(values, scale[pl.ds(b, 1), :], shift[pl.ds(b, 1), :], target, rows, cols)

    def conv(columns, i):
        product = jnp.dot(columns[...], weight_ref[...], preferred_element_type=jnp.float32)
        own = pair_ref[i, 1 : 1 + rows].reshape(inner, lanes).astype(jnp.float32)
        out_ref[i] = spread(product, cols) + own

    @pl.when(step == 0)
    def _():
        gain = jnp.pad(gain_ref[...].astype(jnp.float32), ((0, 0), (0, lanes - chans)))
        group_affine(sums_ref, more_ref, 0, gain, count, group, chans, scale, shift)
        make(pair_ref[0], 0, even)

    make(pair_ref[1], 2 * step + 1, odd)
    conv(even, 0)
    make(next_ref[0], jnp.minimum(2 * step + 2, batch - 1), even)
    conv(odd, 1)


def in_pairs(array):
    rest = (0,) * (array.ndim - 1)
    return pl.BlockSpec((2,) + tuple(array.shape[1:]), lambda b: (b,) + rest)


def next_up(array):
    rest = (0,) * (array.ndim - 1)
    last = array.shape[0] - 1
    return pl.BlockSpec(
        (1,) + tuple(array.shape[1:]), lambda b: (jnp.minimum(2 * b + 2, last),) + rest
    )


def unet_call(sums, more, gain, unet_first, weight, count, group, chans):
    batch, total_rows, cols, lanes = unet_first.shape
    inner = (total_rows - 2) * cols
    depth = weight.shape[0]
    out = jax.ShapeDtypeStruct((batch, inner, lanes), jnp.float32)
    return pl.pallas_call(
        functools.partial(unet_kernel, count=count, group=group, chans=chans),
        grid=(batch // 2,),
        in_specs=[whole(sums), whole(more), whole(gain)]
        + [in_pairs(unet_first), next_up(unet_first), whole(weight)],
        out_specs=in_pairs(out),
        scratch_shapes=[
            pltpu.VMEM((batch, lanes), jnp.float32),
            pltpu.VMEM((batch, lanes), jnp.float32),
            pltpu.VMEM((inner, depth), jnp.bfloat16),
            pltpu.VMEM((inner, depth), jnp.bfloat16),
        ],
        out_shape=out,
        compiler_params=params(24),
        cost_estimate=cost(2 * batch * inner * 1024 * 1024),
        name="unet_conv",
    )(sums, more, gain, unet_first, unet_first, weight)


def control_kernel(
    cond_ref, valid_ref, scale_ref, sums_ref, more_ref, gain_ref, pair_ref, next_ref, a_ref,
    u_ref, base_ref, *rest, nets, count, group, chans,
):
    pieces = rest[: 2 * CHUNKS * nets]
    skip0_ref, skip1_ref, scale, shift, even, odd, weights, heads, sems = rest[
        2 * CHUNKS * nets :
    ]
    step = pl.program_id(0)
    batch = sums_ref.shape[0]
    _, total_rows, cols, lanes = pair_ref.shape
    rows = total_rows - 2
    inner = rows * cols
    main = main_of(chans)
    tail = chans - main
    part = chans // 2
    stem_part = heads.shape[1] // 2

    def segments(n, half):
        yield 0, stem_part, heads, n, half * stem_part
        low, high = half * part, (half + 1) * part
        for dy in range(3):
            first = stem_part + dy * part
            if low < main:
                yield first, min(high, main) - low, weights, n, dy * main + low
            if high > main:
                begin = max(low, main)
                yield (
                    first + begin - low, high - begin, weights, n,
                    3 * main + dy * tail + begin - main,
                )

    def copies(flip):
        made = []
        for n in range(nets):
            for order in range(2):
                bound = 0
                chunks = []
                for piece in pieces[CHUNKS * (2 * n + order) : CHUNKS * (2 * n + order + 1)]:
                    chunks.append((bound, bound + piece.shape[0], piece))
                    bound += piece.shape[0]
                for first, size, target, at, to in segments(n, order ^ flip):
                    for low, high, piece in chunks:
                        start, stop = max(first, low), min(first + size, high)
                        if start < stop:
                            made.append(
                                (
                                    piece.at[
                                        pl.ds(start - low, stop - start),
                                        pl.ds(0, target.shape[2]),
                                    ],
                                    target.at[at, pl.ds(to + start - first, stop - start), :],
                                )
                            )
        return [pltpu.make_async_copy(s, t, sems.at[i]) for i, (s, t) in enumerate(made)]

    def for_side(act):
        for flip in range(2):

            @pl.when((lax.axis_index("rep") & 1) == flip)
            def _():
                for copy in copies(flip):
                    act(copy)

    def make(values, b, target):
        values = values.reshape(total_rows * cols, lanes)
        normed_columns(values, scale[pl.ds(b, 1), :], shift[pl.ds(b, 1), :], target, rows, cols)

    def conv(columns, i):
        b = 2 * step + i
        slot = slot_of(cond_ref[b, 0], nets)
        live = scale_ref[b] * valid_ref[b].astype(jnp.float32)
        heads_out = jnp.dot(a_ref[i], heads[slot], preferred_element_type=jnp.float32)
        own = u_ref[i, 1 : 1 + rows].reshape(inner, lanes).astype(jnp.float32)
        first = own + live * heads_out[:, 0:lanes]
        skip0_ref[i] = first[:, 0:chans].astype(jnp.bfloat16)
        product = jnp.dot(columns[...], weights[slot], preferred_element_type=jnp.float32)
        second = base_ref[i] + live * (spread(product, cols) + heads_out[:, lanes:])
        skip1_ref[i] = second[:, 0:chans].astype(jnp.bfloat16)

    @pl.when(step == 0)
    def _():
        for_side(lambda copy: copy.start())
        for n in range(nets):
            weights[n, 3 * chans :, :] = jnp.zeros(
                (weights.shape[1] - 3 * chans, weights.shape[2]), jnp.bfloat16
            )
        group_affine(sums_ref, more_ref, 1, gain_ref[:, 0, :], count, group, chans, scale, shift)
        make(pair_ref[0], 0, even)
        for_side(lambda copy: copy.wait())

    make(pair_ref[1], 2 * step + 1, odd)
    conv(even, 0)
    make(next_ref[0], jnp.minimum(2 * step + 2, batch - 1), even)
    conv(odd, 1)


def control_call(
    cond_ids, valid, cond_scale, sums, more, gains, control_first, grids, unet_first, base,
    pieces, count, group, chans,
):
    batch, total_rows, cols, lanes = control_first.shape
    inner = (total_rows - 2) * cols
    nets = len(pieces) // (2 * CHUNKS)
    width = pieces[0].shape[1]
    depth = grids.shape[2]
    out = jax.ShapeDtypeStruct((batch, inner, chans), jnp.bfloat16)
    return pl.pallas_call(
        functools.partial(control_kernel, nets=nets, count=count, group=group, chans=chans),
        grid=(batch // 2,),
        in_specs=[whole(array, pltpu.SMEM) for array in (cond_ids, valid, cond_scale)]
        + [whole(sums), whole(more), whole(gains)]
        + [in_pairs(control_first), next_up(control_first)]
        + [in_pairs(array) for array in (grids, unet_first, base)]
        + [whole(array, pl.ANY) for array in pieces],
        out_specs=[in_pairs(out), in_pairs(out)],
        scratch_shapes=[
            pltpu.VMEM((batch, lanes), jnp.float32),
            pltpu.VMEM((batch, lanes), jnp.float32),
            pltpu.VMEM((inner, width), jnp.bfloat16),
            pltpu.VMEM((inner, width), jnp.bfloat16),
            pltpu.VMEM((nets, width, width), jnp.bfloat16),
            pltpu.VMEM((nets, depth, 2 * lanes), jnp.bfloat16),
            pltpu.SemaphoreType.DMA((16 * CHUNKS * nets,)),
        ],
        out_shape=[out, out],
        compiler_params=params(24 + 3 * nets),
        cost_estimate=cost(2 * batch * inner * 1024 * 1280),
        name="control_conv",
    )(
        cond_ids, valid, cond_scale, sums, more, gains, control_first, control_first, grids,
        unet_first, base, *pieces,
    )


def shards(
    latent, hint, cond_ids, valid, cond_scale,
    ctl_in, ctl_hint, ctl_zero0, ctl_gain, ctl_conv, ctl_zero1,
    unet_in, unet_gain, unet_conv,
):
    batch, rows, flat = latent.shape
    cols = flat // LCH
    nets = lax.axis_size("net")
    reps = lax.axis_size("rep")
    chans = unet_gain.shape[0]
    group = chans // GROUPS
    count = rows * reps * cols * group
    depth = up_to(hint.shape[3] + 9 * LCH, 256)

    def moved(arrays, axis, pairs):
        got = []
        for array in arrays:
            got.append(lax.ppermute(array, axis, pairs))
        return got

    def along_net(arrays, offset):
        ring = [(n, (n + 2 * offset) % nets) for n in range(nets)]
        return moved(arrays, "net", ring)

    def across(arrays):
        return moved(arrays, "net", [(n, n ^ 1) for n in range(nets)])

    def beside(arrays, bit=1):
        return moved(arrays, "rep", [(r, r ^ bit) for r in range(reps)])

    small = [ctl_in, ctl_gain, ctl_hint]
    far = [along_net(small, s) for s in range(1, nets // 2)]
    stems = small + across(small)
    for got in far:
        stems += got + across(got)

    def edge(hint_row, lat_rows):
        wide = jnp.pad(hint_row, ((0, 0), (0, 0), (0, flat - hint_row.shape[2])))
        return jnp.pad(jnp.concatenate([wide, lat_rows], axis=1), ((0, 0), (0, 6), (0, 0)))

    down = [(r, r + 1) for r in range(reps - 1)]
    up = [(r + 1, r) for r in range(reps - 1)]
    (top,) = moved([edge(hint[:, rows - 1], latent[:, rows - 2 :])], "rep", down)
    (bot,) = moved([edge(hint[:, 0], latent[:, :2])], "rep", up)

    own = compose(ctl_conv, ctl_hint, ctl_in, ctl_zero0, ctl_zero1, depth)
    away = [along_net(own[:CHUNKS], s) for s in range(1, nets // 2)]
    pieces = list(own) + across(own)
    for got in away:
        full = got + beside(got)
        pieces += full + across(full)

    unet_first, control_first, grids, sums, gains = stem_call(
        cond_ids, latent, hint, top, bot, unet_in, stems, depth
    )
    step = 1
    while 2 * step < reps:
        sums = sums + beside([sums], step)[0]
        step *= 2
    more = beside([sums], step)[0]

    weight = arrange(unet_conv)
    base = unet_call(sums, more, unet_gain[None], unet_first, weight, count, group, chans)
    skip0, skip1 = control_call(
        cond_ids, valid, cond_scale, sums, more, gains, control_first, grids, unet_first, base,
        pieces, count, group, chans,
    )
    shape = (batch, rows, cols, chans)
    return skip0.reshape(shape), skip1.reshape(shape)


def solution(mesh):
    return placed_over(mesh)


def placed_over(mesh):
    return jax.shard_map(
        shards,
        mesh=mesh,
        in_specs=(
            P("net", "rep", None),
            P("net", "rep", None, None),
            P("net", None),
            P("net"),
            P("net"),
            P("net", None, None, None, None),
            P("net", None, None),
            P("net", None, None),
            P("net", None),
            P("net", None, None, None, None),
            P("net", None, None),
            P(),
            P(),
            P(),
        ),
        out_specs=(P("net", "rep", None, None), P("net", "rep", None, None)),
        check_vma=False,
    )
```

time: 458 us -> 133 us (0.29); the launches traced: 452 us -> 132 us
  matrix products: 232 us -> 0 us
  blocking collectives: 99.9 us -> 0 us
  Pallas kernels: 0 us -> 50.7 us
  local copies, waits for them, and re-layouts: 58.2 us -> 17.1 us
  waiting for transfers between devices: 3.7 us -> 36.9 us
  other arithmetic: 28.8 us -> 0.13 us
  between operations: 14.7 us -> 1.08 us
  starting transfers between devices: 15 us -> 26.2 us
    dot_general x38 -> x0, matrix products: 232 us -> none  [the longest x18 110 us: conv_rows(): jnp.dot(window.reshape(-1, window.shape[-1]), weight[shift_y, shift_x], p...]
    all_gather x5 -> x0, blocking collectives: 54.5 us -> none  [the longest x1 16.1 us: shards(): lax.all_gather(ctl_zero1, 'net', axis=0, tiled=True)]
    pallas_call x0 -> x5, Pallas kernels: none -> 50.7 us  [the longest x1 25.9 us: control_call(): pl.pallas_call(functools.partial(control_kernel, nets=nets, count=count,...]
    psum x1 -> x0, blocking collectives: 45.3 us -> none  [unet_sums(): return lax.psum((totals[0], totals[1]), 'rep')]
    gather x11 -> x0, local copies, waits for them, and re-layouts: 43 us -> none  [shards(): jnp.take(stacked, cond_idx, axis=0)]
    ppermute x6 -> x32, waiting for transfers between devices: 3.68 us -> 36.9 us  [moved(): got.append(lax.ppermute(array, axis, pairs))]
    select_n x4 -> x0, other arithmetic: 12.6 us -> none  [shards(): jnp.take(stacked, cond_idx, axis=0)]
    ppermute x6 -> x32, starting transfers between devices: 15 us -> 26.2 us  [moved(): got.append(lax.ppermute(array, axis, pairs))]
  transfers between devices with their start and end apart: 7 -> 32, of which waited for: 1 -> 8; matrix products, arithmetic and copies ran while one was open for 39% -> 3% of each run, Pallas kernels for 0% -> 19%
where the time goes in v1:
time: 133 us; the launch traced here: 132 us
  Pallas kernels  50.7 us (38%)
  waiting for transfers between devices  36.9 us (28%)
  starting transfers between devices  26.2 us (20%)
  local copies, waits for them, and re-layouts  17.1 us (13%)
    ppermute x32, waiting for transfers between devices, moved(): got.append(lax.ppermute(array, axis, pairs))  36.9 us
    ppermute x32, starting transfers between devices, moved(): got.append(lax.ppermute(array, axis, pairs))  26.2 us
    pallas_call x1, Pallas kernels, control_call(): pl.pallas_call(functools.partial(control_kernel, nets=nets, count=count,...  25.9 us
    unnamed x63, local copies, waits for them, and re-layouts  13.7 us
    pallas_call x1, Pallas kernels, unet_call(): pl.pallas_call(functools.partial(unet_kernel, count=count, group=group, c...  11.2 us
    pallas_call x1, Pallas kernels, stem_call(): pl.pallas_call(functools.partial(stem_kernel, nets=nets), grid=(batch,),...  8.76 us
    pallas_call x1, Pallas kernels, compose(): pl.pallas_call(compose_kernel, in_specs=[pl.BlockSpec(memory_space=pltpu....  4.01 us
  transfers between devices with their start and end apart: 32, of which 8 were waited for; matrix products, arithmetic and copies ran while one was open for 3% of the time, Pallas kernels for 19%

profile of v1, /device:TPU:0, one launch (start us, length us, event | category | flops | bytes accessed | tf_op | source)
XLA Modules:
  0.0 132.1 jit_solution(10583825094926873353)
XLA Ops:
  0.7 3.0 %collective-permute-start.7 = (bf16[1,192,320]{2,1,0:T(8,128)(2,1)}, bf16[1,192,320]{2,1,0:T(8,128)(2,1)S(1)}, u32[]{:S(2)}, u32[]{:S(2)}) collective-permute-start(bf16[1,192,320]{2,1,0:T(8,128)(2,1)} %refs_1_.1), channel_id=1, source_target_pairs={{0,16},{8,24},{16,0},{24,8},{1,17},{9,25},{17,1},{25,9},{2,18},{10... | collective-permute-start | bytes 368648 | tf_op jit(solution)/shard_map/ppermute | solution.py:576
  4.6 1.1 slice_bitcast_fusion
  6.5 4.1 %collective-permute-start = (bf16[8,72,256]{2,1,0:T(8,128)(2,1)}, bf16[8,72,256]{2,1,0:T(8,128)(2,1)}, u32[]{:S(2)}, u32[]{:S(2)}) collective-permute-start(bf16[8,72,256]{2,1,0:T(8,128)(2,1)} %pad.15), channel_id=1, source_target_pairs={{0,1},{1,2},{2,3},{3,4},{4,5},{5,6},{6,7},{8,9},{9,10},{10,11},{11... | collective-permute-start | bytes 884744 | tf_op jit(solution)/shard_map/ppermute | solution.py:576
  11.4 1.4 %collective-permute-start.1 = (bf16[8,72,256]{2,1,0:T(8,128)(2,1)}, bf16[8,72,256]{2,1,0:T(8,128)(2,1)}, u32[]{:S(2)}, u32[]{:S(2)}) collective-permute-start(bf16[8,72,256]{2,1,0:T(8,128)(2,1)} %pad.17), channel_id=1, source_target_pairs={{1,0},{2,1},{3,2},{4,3},{5,4},{6,5},{7,6},{9,8},{10,9},{11,10},{12... | collective-permute-start | bytes 884744 | tf_op jit(solution)/shard_map/ppermute | solution.py:576
  13.6 2.8 %collective-permute-done.6.rest_7_ = bf16[1,320]{1,0:T(2,128)(2,1)S(1)} collective-permute-done((bf16[1,320]{1,0:T(2,128)(2,1)S(1)}, bf16[1,320]{1,0:T(2,128)(2,1)S(1)}, u32[]{:S(2)}, u32[]{:S(2)}) %collective-permute-start.6) | collective-permute-done | bytes 672 | tf_op jit(solution)/shard_map/ppermute | solution.py:576
  19.2 2.3 %collective-permute-done.5.rest_6_ = bf16[1,3,3,4,320]{4,3,2,1,0:T(4,128)(2,1)S(1)} collective-permute-done((bf16[1,3,3,4,320]{4,3,2,1,0:T(4,128)(2,1)S(1)}, bf16[1,3,3,4,320]{4,3,2,1,0:T(4,128)(2,1)S(1)}, u32[]{:S(2)}, u32[]{:S(2)}) %collective-permute-start.5) | collective-permute-done | bytes 23072 | tf_op jit(solution)/shard_map/ppermute | solution.py:576
  22.1 4.0 %compose.1 = (bf16[208,1024]{1,0:T(8,128)(2,1)S(1)}, bf16[208,1024]{1,0:T(8,128)(2,1)S(1)}, bf16[192,1024]{1,0:T(8,128)(2,1)}, bf16[208,1024]{1,0:T(8,128)(2,1)S...) custom-call(bf16[1,3,3,320,320]{4,3,2,1,0:T(8,128)(2,1)S(1)} %copy-done.3, ...), custom_call_target="tpu_custom_call" | custom-call | flops 1593835520 | bytes 1048576 | tf_op jit(solution)/shard_map/compose/pallas_call | solution.py:111
  30.2 1.1 copy-done.9
  31.3 0.9 copy-done.11
  33.1 0.9 copy-done.15
  36.7 8.8 %stem.1 = (bf16[8,10,64,384]{3,2,1,0:T(8,128)(2,1)S(1)}, bf16[8,10,64,384]{3,2,1,0:T(8,128)(2,1)S(1)}, bf16[8,512,256]{2,1,0:T(8,128)(2,1)S(1)}, f32[8,4,384]{2,1,0:T(4,128)S(1)}, f32[8,1,384]{2,1,0:T(1,128)S(1)}) custom-call(s32[8,1]{1,0:T(8,128)S(1)} %copy.19.cond_ref, bf16[8,8,256]{2,1,0:T(8,128)(2,1)S(1)} %copy-done.2, ...), custom_call_target="tpu_custom_call" | custom-call | flops 2348810240 | bytes 1048576 | tf_op jit(solution)/shard_map/stem/pallas_call | solution.py:273
  45.4 2.7 %collective-permute-start.11 = (f32[8,4,384]{2,1,0:T(4,128)S(1)}, f32[8,4,384]{2,1,0:T(4,128)S(1)}, u32[]{:S(2)}, u32[]{:S(2)}) collective-permute-start(f32[8,4,384]{2,1,0:T(4,128)S(1)} %get-tuple-element.15), channel_id=1, source_target_pairs={{0,1},{1,0},{2,3},{3,2},{4,5},{5,4},{6,7},{7,6},{8,9},{9,8},{10,11... | collective-permute-start | bytes 147464 | tf_op jit(solution)/shard_map/ppermute | solution.py:576
  48.4 2.2 %collective-permute-done.11 = f32[8,4,384]{2,1,0:T(4,128)S(1)} collective-permute-done((f32[8,4,384]{2,1,0:T(4,128)S(1)}, f32[8,4,384]{2,1,0:T(4,128)S(1)}, u32[]{:S(2)}, u32[]{:S(2)}) %collective-permute-start.11) | collective-permute-done | bytes 49184 | tf_op jit(solution)/shard_map/ppermute | solution.py:576
  50.6 2.0 %collective-permute-start.12 = (f32[8,4,384]{2,1,0:T(4,128)S(1)}, f32[8,4,384]{2,1,0:T(4,128)S(1)}, u32[]{:S(2)}, u32[]{:S(2)}) collective-permute-start(f32[8,4,384]{2,1,0:T(4,128)S(1)} %add.14), channel_id=1, source_target_pairs={{0,2},{1,3},{2,0},{3,1},{4,6},{5,7},{6,4},{7,5},{8,10},{9,11},{10,... | collective-permute-start | bytes 147464 | tf_op jit(solution)/shard_map/ppermute | solution.py:576
  52.7 1.3 collective-permute-start.20
  55.3 10.1 %collective-permute-done.20.rest_12_ = bf16[208,1024]{1,0:T(8,128)(2,1)S(1)} collective-permute-done((bf16[208,1024]{1,0:T(8,128)(2,1)S(1)}, bf16[208,1024]{1,0:T(8,128)(2,1)S(1)}, u32[]{:S(2)}, u32[]{:S(2)}) %collective-permute-start.20) | collective-permute-done | bytes 426016 | tf_op jit(solution)/shard_map/ppermute | solution.py:576
  66.0 6.9 %collective-permute-done.21.rest_13_ = bf16[208,1024]{1,0:T(8,128)(2,1)S(1)} collective-permute-done((bf16[208,1024]{1,0:T(8,128)(2,1)S(1)}, bf16[208,1024]{1,0:T(8,128)(2,1)S(1)}, u32[]{:S(2)}, u32[]{:S(2)}) %collective-permute-start.21) | collective-permute-done | bytes 426016 | tf_op jit(solution)/shard_map/ppermute | solution.py:576
  73.5 1.4 %collective-permute-start.25 = (bf16[192,1024]{1,0:T(8,128)(2,1)}, bf16[192,1024]{1,0:T(8,128)(2,1)S(1)}, u32[]{:S(2)}, u32[]{:S(2)}) collective-permute-start(bf16[192,1024]{1,0:T(8,128)(2,1)} %collective-permute-done.22.rest_14_), channel_id=1, source_target_pairs={{0,1},{1,0},{2,3},{3,2},{4,5},{5,4},{6,7},{7,6},{8,9},{9,8},{10,11... | collective-permute-start | bytes 1179656 | tf_op jit(solution)/shard_map/ppermute | solution.py:576
  75.0 2.6 %collective-permute-start.13 = (f32[8,4,384]{2,1,0:T(4,128)S(1)}, f32[8,4,384]{2,1,0:T(4,128)S(1)}, u32[]{:S(2)}, u32[]{:S(2)}) collective-permute-start(f32[8,4,384]{2,1,0:T(4,128)S(1)} %add.15.sums_ref), channel_id=1, source_target_pairs={{0,4},{1,5},{2,6},{3,7},{4,0},{5,1},{6,2},{7,3},{8,12},{9,13},{10,... | collective-permute-start | bytes 147464 | tf_op jit(solution)/shard_map/ppermute | solution.py:576
  78.5 2.2 %collective-permute-done.13.more_ref = f32[8,4,384]{2,1,0:T(4,128)S(1)} collective-permute-done((f32[8,4,384]{2,1,0:T(4,128)S(1)}, f32[8,4,384]{2,1,0:T(4,128)S(1)}, u32[]{:S(2)}, u32[]{:S(2)}) %collective-permute-start.13) | collective-permute-done | bytes 49184 | tf_op jit(solution)/shard_map/ppermute | solution.py:576
  81.2 10.4 %collective-permute-done.25.rest_17_ = bf16[192,1024]{1,0:T(8,128)(2,1)S(1)} collective-permute-done((bf16[192,1024]{1,0:T(8,128)(2,1)}, bf16[192,1024]{1,0:T(8,128)(2,1)S(1)}, u32[]{:S(2)}, u32[]{:S(2)}) %collective-permute-start.25) | collective-permute-done | bytes 393248 | tf_op jit(solution)/shard_map/ppermute | solution.py:576
  92.2 11.2 %unet_conv.1.base_ref = f32[8,512,384]{2,1,0:T(8,128)S(1)} custom-call(f32[8,4,384]{2,1,0:T(4,128)S(1)} %add.15.sums_ref, f32[8,4,384]{2,1,0:T(4,128)S(1)} %collective-permute-done.13.more_ref, bf16[1,320]{1,0:T(2,128)(2,1)S(1)} %broadcast_in_dim.3.gain_ref, bf16[8,10,64,384]{3,2,1,0:T(8,128)(2,1)S(1)} %get-tuple-element.19.pair_ref.next_ref.u_ref, ...), custom_call_target="tpu_custom_call" | custom-call | flops 8589934592 | bytes 1048576 | tf_op jit(solution)/shard_map/unet_conv/pallas_call | solution.py:405
  103.4 2.6 %copy-done.29 = f32[8,512,384]{2,1,0:T(8,128)} copy-done((f32[8,512,384]{2,1,0:T(8,128)}, f32[8,512,384]{2,1,0:T(8,128)S(1)}, u32[]{:S(2)}) %copy-start.29) | copy-done | bytes 6291480
  106.1 25.9 %control_conv.1 = (bf16[8,512,320]{2,1,0:T(8,128)(2,1)}, bf16[8,512,320]{2,1,0:T(8,128)(2,1)}) custom-call(s32[8,1]{1,0:T(8,128)S(1)} %copy.19.cond_ref, s32[8]{0:T(128)S(1)} %copy-done.26, f32[8]{0:T(128)S(1)} %copy-done.27, f32[8,4,384]{2,1,0:T(4,128)S(1)} %add.15.sums_ref, f32[8,4,384]{2,1,0:T(4,128)S(1)} %collective-permute-done.13.more_ref, ...), custom_call_target="tpu_custom_call" | custom-call | flops 10737418240 | bytes 1048576 | tf_op jit(solution)/shard_map/control_conv/pallas_call | solution.py:531
  (117 shorter events, 19.1 us)
Async XLA Ops:
  0.7 21.3 %collective-permute-start.7 = (bf16[1,192,320]{2,1,0:T(8,128)(2,1)}, bf16[1,192,320]{2,1,0:T(8,128)(2,1)S(1)}, u32[]{:S(2)}, u32[]{:S(2)}) collective-permute-start(bf16[1,192,320]{2,1,0:T(8,128)(2,1)} %refs_1_.1), channel_id=1, source_target_pairs={{0,16},{8,24},{16,0},{24,8},{1,17},{9,25},{17,1},{25,9},{2,18},{10... | collective-permute-start | bytes 368648 | tf_op jit(solution)/shard_map/ppermute | solution.py:576
  6.5 23.7 %collective-permute-start = (bf16[8,72,256]{2,1,0:T(8,128)(2,1)}, bf16[8,72,256]{2,1,0:T(8,128)(2,1)}, u32[]{:S(2)}, u32[]{:S(2)}) collective-permute-start(bf16[8,72,256]{2,1,0:T(8,128)(2,1)} %pad.15), channel_id=1, source_target_pairs={{0,1},{1,2},{2,3},{3,4},{4,5},{5,6},{6,7},{8,9},{9,10},{10,11},{11... | collective-permute-start | bytes 884744 | tf_op jit(solution)/shard_map/ppermute | solution.py:576
  11.4 18.8 %collective-permute-start.1 = (bf16[8,72,256]{2,1,0:T(8,128)(2,1)}, bf16[8,72,256]{2,1,0:T(8,128)(2,1)}, u32[]{:S(2)}, u32[]{:S(2)}) collective-permute-start(bf16[8,72,256]{2,1,0:T(8,128)(2,1)} %pad.17), channel_id=1, source_target_pairs={{1,0},{2,1},{3,2},{4,3},{5,4},{6,5},{7,6},{9,8},{10,9},{11,10},{12... | collective-permute-start | bytes 884744 | tf_op jit(solution)/shard_map/ppermute | solution.py:576
  21.5 5.8 %collective-permute-start.4 = (bf16[1,192,320]{2,1,0:T(8,128)(2,1)S(1)}, bf16[1,192,320]{2,1,0:T(8,128)(2,1)S(1)}, u32[]{:S(2)}, u32[]{:S(2)}) collective-permute-start(bf16[1,192,320]{2,1,0:T(8,128)(2,1)S(1)} %copy-done.8), channel_id=1, source_target_pairs={{0,8},{8,0},{16,24},{24,16},{1,9},{9,1},{17,25},{25,17},{2,10},{10... | collective-permute-start | bytes 368648 | tf_op jit(solution)/shard_map/ppermute | solution.py:576
  22.0 6.8 %collective-permute-start.10 = (bf16[1,192,320]{2,1,0:T(8,128)(2,1)S(1)}, bf16[1,192,320]{2,1,0:T(8,128)(2,1)S(1)}, u32[]{:S(2)}, u32[]{:S(2)}) collective-permute-start(bf16[1,192,320]{2,1,0:T(8,128)(2,1)S(1)} %collective-permute-done.7.rest_8_), channel_id=1, source_target_pairs={{0,8},{8,0},{16,24},{24,16},{1,9},{9,1},{17,25},{25,17},{2,10},{10... | collective-permute-start | bytes 368648 | tf_op jit(solution)/shard_map/ppermute | solution.py:576
  26.9 25.8 %collective-permute-start.19 = (bf16[192,1024]{1,0:T(8,128)(2,1)}, bf16[192,1024]{1,0:T(8,128)(2,1)}, u32[]{:S(2)}, u32[]{:S(2)}) collective-permute-start(bf16[192,1024]{1,0:T(8,128)(2,1)} %get-tuple-element.25.rest_5_), channel_id=1, source_target_pairs={{0,8},{8,0},{16,24},{24,16},{1,9},{9,1},{17,25},{25,17},{2,10},{10... | collective-permute-start | bytes 1179656 | tf_op jit(solution)/shard_map/ppermute | solution.py:576
  28.0 25.9 %collective-permute-start.22 = (bf16[192,1024]{1,0:T(8,128)(2,1)}, bf16[192,1024]{1,0:T(8,128)(2,1)}, u32[]{:S(2)}, u32[]{:S(2)}) collective-permute-start(bf16[192,1024]{1,0:T(8,128)(2,1)} %get-tuple-element.22.rest_2_), channel_id=1, source_target_pairs={{0,16},{8,24},{16,0},{24,8},{1,17},{9,25},{17,1},{25,9},{2,18},{10... | collective-permute-start | bytes 1179656 | tf_op jit(solution)/shard_map/ppermute | solution.py:576
  29.4 25.3 %collective-permute-start.16 = (bf16[192,1024]{1,0:T(8,128)(2,1)}, bf16[192,1024]{1,0:T(8,128)(2,1)}, u32[]{:S(2)}, u32[]{:S(2)}) collective-permute-start(bf16[192,1024]{1,0:T(8,128)(2,1)} %get-tuple-element.22.rest_2_), channel_id=1, source_target_pairs={{0,8},{8,0},{16,24},{24,16},{1,9},{9,1},{17,25},{25,17},{2,10},{10... | collective-permute-start | bytes 1179656 | tf_op jit(solution)/shard_map/ppermute | solution.py:576
  48.2 7.0 %collective-permute-start.17 = (bf16[208,1024]{1,0:T(8,128)(2,1)S(1)}, bf16[208,1024]{1,0:T(8,128)(2,1)S(1)}, u32[]{:S(2)}, u32[]{:S(2)}) collective-permute-start(bf16[208,1024]{1,0:T(8,128)(2,1)S(1)} %get-tuple-element.23.rest_3_), channel_id=1, source_target_pairs={{0,8},{8,0},{16,24},{24,16},{1,9},{9,1},{17,25},{25,17},{2,10},{10... | collective-permute-start | bytes 1277960 | tf_op jit(solution)/shard_map/ppermute | solution.py:576
  52.7 12.7 %collective-permute-start.20 = (bf16[208,1024]{1,0:T(8,128)(2,1)S(1)}, bf16[208,1024]{1,0:T(8,128)(2,1)S(1)}, u32[]{:S(2)}, u32[]{:S(2)}) collective-permute-start(bf16[208,1024]{1,0:T(8,128)(2,1)S(1)} %get-tuple-element.20.rest_0_), channel_id=1, source_target_pairs={{0,16},{8,24},{16,0},{24,8},{1,17},{9,25},{17,1},{25,9},{2,18},{10... | collective-permute-start | bytes 1277960 | tf_op jit(solution)/shard_map/ppermute | solution.py:576
  53.9 19.0 %collective-permute-start.21 = (bf16[208,1024]{1,0:T(8,128)(2,1)S(1)}, bf16[208,1024]{1,0:T(8,128)(2,1)S(1)}, u32[]{:S(2)}, u32[]{:S(2)}) collective-permute-start(bf16[208,1024]{1,0:T(8,128)(2,1)S(1)} %get-tuple-element.21.rest_1_), channel_id=1, source_target_pairs={{0,16},{8,24},{16,0},{24,8},{1,17},{9,25},{17,1},{25,9},{2,18},{10... | collective-permute-start | bytes 1277960 | tf_op jit(solution)/shard_map/ppermute | solution.py:576
  54.7 18.8 %collective-permute-start.18 = (bf16[208,1024]{1,0:T(8,128)(2,1)S(1)}, bf16[208,1024]{1,0:T(8,128)(2,1)S(1)}, u32[]{:S(2)}, u32[]{:S(2)}) collective-permute-start(bf16[208,1024]{1,0:T(8,128)(2,1)S(1)} %copy-done.5), channel_id=1, source_target_pairs={{0,8},{8,0},{16,24},{24,16},{1,9},{9,1},{17,25},{25,17},{2,10},{10... | collective-permute-start | bytes 1277960 | tf_op jit(solution)/shard_map/ppermute | solution.py:576
  54.8 18.8 %collective-permute-start.14 = (bf16[208,1024]{1,0:T(8,128)(2,1)S(1)}, bf16[208,1024]{1,0:T(8,128)(2,1)S(1)}, u32[]{:S(2)}, u32[]{:S(2)}) collective-permute-start(bf16[208,1024]{1,0:T(8,128)(2,1)S(1)} %get-tuple-element.20.rest_0_), channel_id=1, source_target_pairs={{0,8},{8,0},{16,24},{24,16},{1,9},{9,1},{17,25},{25,17},{2,10},{10... | collective-permute-start | bytes 1277960 | tf_op jit(solution)/shard_map/ppermute | solution.py:576
  55.2 19.8 %collective-permute-start.15 = (bf16[208,1024]{1,0:T(8,128)(2,1)S(1)}, bf16[208,1024]{1,0:T(8,128)(2,1)S(1)}, u32[]{:S(2)}, u32[]{:S(2)}) collective-permute-start(bf16[208,1024]{1,0:T(8,128)(2,1)S(1)} %get-tuple-element.21.rest_1_), channel_id=1, source_target_pairs={{0,8},{8,0},{16,24},{24,16},{1,9},{9,1},{17,25},{25,17},{2,10},{10... | collective-permute-start | bytes 1277960 | tf_op jit(solution)/shard_map/ppermute | solution.py:576
  65.3 26.2 %collective-permute-start.23 = (bf16[208,1024]{1,0:T(8,128)(2,1)S(1)}, bf16[208,1024]{1,0:T(8,128)(2,1)S(1)}, u32[]{:S(2)}, u32[]{:S(2)}) collective-permute-start(bf16[208,1024]{1,0:T(8,128)(2,1)S(1)} %collective-permute-done.20.rest_12_), channel_id=1, source_target_pairs={{0,1},{1,0},{2,3},{3,2},{4,5},{5,4},{6,7},{7,6},{8,9},{9,8},{10,11... | collective-permute-start | bytes 1277960 | tf_op jit(solution)/shard_map/ppermute | solution.py:576
  72.9 19.2 %collective-permute-start.24 = (bf16[208,1024]{1,0:T(8,128)(2,1)S(1)}, bf16[208,1024]{1,0:T(8,128)(2,1)S(1)}, u32[]{:S(2)}, u32[]{:S(2)}) collective-permute-start(bf16[208,1024]{1,0:T(8,128)(2,1)S(1)} %collective-permute-done.21.rest_13_), channel_id=1, source_target_pairs={{0,1},{1,0},{2,3},{3,2},{4,5},{5,4},{6,7},{7,6},{8,9},{9,8},{10,11... | collective-permute-start | bytes 1277960 | tf_op jit(solution)/shard_map/ppermute | solution.py:576
  73.5 7.1 %collective-permute-start.28 = (bf16[192,1024]{1,0:T(8,128)(2,1)}, bf16[192,1024]{1,0:T(8,128)(2,1)S(1)}, u32[]{:S(2)}, u32[]{:S(2)}) collective-permute-start(bf16[192,1024]{1,0:T(8,128)(2,1)} %collective-permute-done.22.rest_14_), channel_id=1, source_target_pairs={{0,8},{8,0},{16,24},{24,16},{1,9},{9,1},{17,25},{25,17},{2,10},{10... | collective-permute-start | bytes 1179656 | tf_op jit(solution)/shard_map/ppermute | solution.py:576
  73.5 18.0 %collective-permute-start.25 = (bf16[192,1024]{1,0:T(8,128)(2,1)}, bf16[192,1024]{1,0:T(8,128)(2,1)S(1)}, u32[]{:S(2)}, u32[]{:S(2)}) collective-permute-start(bf16[192,1024]{1,0:T(8,128)(2,1)} %collective-permute-done.22.rest_14_), channel_id=1, source_target_pairs={{0,1},{1,0},{2,3},{3,2},{4,5},{5,4},{6,7},{7,6},{8,9},{9,8},{10,11... | collective-permute-start | bytes 1179656 | tf_op jit(solution)/shard_map/ppermute | solution.py:576
  75.0 5.7 %collective-permute-start.13 = (f32[8,4,384]{2,1,0:T(4,128)S(1)}, f32[8,4,384]{2,1,0:T(4,128)S(1)}, u32[]{:S(2)}, u32[]{:S(2)}) collective-permute-start(f32[8,4,384]{2,1,0:T(4,128)S(1)} %add.15.sums_ref), channel_id=1, source_target_pairs={{0,4},{1,5},{2,6},{3,7},{4,0},{5,1},{6,2},{7,3},{8,12},{9,13},{10,... | collective-permute-start | bytes 147464 | tf_op jit(solution)/shard_map/ppermute | solution.py:576
  80.7 25.4 %collective-permute-start.26 = (bf16[208,1024]{1,0:T(8,128)(2,1)S(1)}, bf16[208,1024]{1,0:T(8,128)(2,1)S(1)}, u32[]{:S(2)}, u32[]{:S(2)}) collective-permute-start(bf16[208,1024]{1,0:T(8,128)(2,1)S(1)} %collective-permute-done.20.rest_12_), channel_id=1, source_target_pairs={{0,8},{8,0},{16,24},{24,16},{1,9},{9,1},{17,25},{25,17},{2,10},{10... | collective-permute-start | bytes 1277960 | tf_op jit(solution)/shard_map/ppermute | solution.py:576
  80.7 25.4 %collective-permute-start.27 = (bf16[208,1024]{1,0:T(8,128)(2,1)S(1)}, bf16[208,1024]{1,0:T(8,128)(2,1)S(1)}, u32[]{:S(2)}, u32[]{:S(2)}) collective-permute-start(bf16[208,1024]{1,0:T(8,128)(2,1)S(1)} %collective-permute-done.21.rest_13_), channel_id=1, source_target_pairs={{0,8},{8,0},{16,24},{24,16},{1,9},{9,1},{17,25},{25,17},{2,10},{10... | collective-permute-start | bytes 1277960 | tf_op jit(solution)/shard_map/ppermute | solution.py:576
  91.6 14.5 %collective-permute-start.31 = (bf16[192,1024]{1,0:T(8,128)(2,1)S(1)}, bf16[192,1024]{1,0:T(8,128)(2,1)S(1)}, u32[]{:S(2)}, u32[]{:S(2)}) collective-permute-start(bf16[192,1024]{1,0:T(8,128)(2,1)S(1)} %collective-permute-done.25.rest_17_), channel_id=1, source_target_pairs={{0,8},{8,0},{16,24},{24,16},{1,9},{9,1},{17,25},{25,17},{2,10},{10... | collective-permute-start | bytes 1179656 | tf_op jit(solution)/shard_map/ppermute | solution.py:576
  91.6 14.5 %collective-permute-start.29 = (bf16[208,1024]{1,0:T(8,128)(2,1)S(1)}, bf16[208,1024]{1,0:T(8,128)(2,1)S(1)}, u32[]{:S(2)}, u32[]{:S(2)}) collective-permute-start(bf16[208,1024]{1,0:T(8,128)(2,1)S(1)} %collective-permute-done.23.rest_15_), channel_id=1, source_target_pairs={{0,8},{8,0},{16,24},{24,16},{1,9},{9,1},{17,25},{25,17},{2,10},{10... | collective-permute-start | bytes 1277960 | tf_op jit(solution)/shard_map/ppermute | solution.py:576
  92.1 14.0 %collective-permute-start.30 = (bf16[208,1024]{1,0:T(8,128)(2,1)S(1)}, bf16[208,1024]{1,0:T(8,128)(2,1)S(1)}, u32[]{:S(2)}, u32[]{:S(2)}) collective-permute-start(bf16[208,1024]{1,0:T(8,128)(2,1)S(1)} %collective-permute-done.24.rest_16_), channel_id=1, source_target_pairs={{0,8},{8,0},{16,24},{24,16},{1,9},{9,1},{17,25},{25,17},{2,10},{10... | collective-permute-start | bytes 1277960 | tf_op jit(solution)/shard_map/ppermute | solution.py:576
  (39 other events, 405.4 us)

commit v2 on v1

--- a/solution.py
+++ b/solution.py
@@ -48,10 +48,10 @@
             target[low : low + LCH, :] = in_weight[dy, dx].astype(jnp.float32)
 
 
-def compose_kernel(*refs):
-    sources, outs = refs[:5], refs[5 : 5 + 2 * CHUNKS]
+def compose_kernel(*refs, order):
+    sources, outs = refs[:5], refs[5 : 5 + CHUNKS]
     conv_ref, hint_ref, in_ref, zero0_ref, zero1_ref, stem, both, whole_half, sems = refs[
-        5 + 2 * CHUNKS :
+        5 + CHUNKS :
     ]
     copies = [
         pltpu.make_async_copy(src.at[0], dst, sems.at[i])
@@ -75,26 +75,25 @@
     second_main = both[:, lanes : lanes + main]
     second_tail = both[:, lanes + main : 2 * lanes]
     stem_part = stem.shape[0] // 2
-    for order in range(2):
-        half = (lax.axis_index("rep") & 1) ^ order
-        lhs = stem[pl.ds(half * stem_part, stem_part), :].astype(jnp.bfloat16)
-        heads = jnp.dot(lhs, both[...], preferred_element_type=jnp.float32)
-        whole_half[0:stem_part, :] = heads.astype(jnp.bfloat16)
-
-        def put(at, width, values):
-            whole_half[stem_part:, at : at + width] = values.astype(jnp.bfloat16)
-
-        tails = []
-        for dx in range(3):
-            lhs = conv_ref[:, dx, pl.ds(half * part, part), :].reshape(3 * part, chans)
-            put(dx * main, main, jnp.dot(lhs, second_main, preferred_element_type=jnp.float32))
-            tails.append(jnp.dot(lhs, second_tail, preferred_element_type=jnp.float32))
-        put(3 * main, LANES, tails[0] + pltpu.roll(tails[1], LANES // 2, 1))
-        put(3 * main + LANES, LANES, tails[2])
-        low = 0
-        for out in outs[CHUNKS * order : CHUNKS * (order + 1)]:
-            out[...] = whole_half[low : low + out.shape[0], :]
-            low += out.shape[0]
+    half = (lax.axis_index("rep") & 1) ^ order
+    lhs = stem[pl.ds(half * stem_part, stem_part), :].astype(jnp.bfloat16)
+    heads = jnp.dot(lhs, both[...], preferred_element_type=jnp.float32)
+    whole_half[0:stem_part, :] = heads.astype(jnp.bfloat16)
+
+    def put(at, width, values):
+        whole_half[stem_part:, at : at + width] = values.astype(jnp.bfloat16)
+
+    tails = []
+    for dx in range(3):
+        lhs = conv_ref[:, dx, pl.ds(half * part, part), :].reshape(3 * part, chans)
+        put(dx * main, main, jnp.dot(lhs, second_main, preferred_element_type=jnp.float32))
+        tails.append(jnp.dot(lhs, second_tail, preferred_element_type=jnp.float32))
+    put(3 * main, LANES, tails[0] + pltpu.roll(tails[1], LANES // 2, 1))
+    put(3 * main + LANES, LANES, tails[2])
+    low = 0
+    for out in outs:
+        out[...] = whole_half[low : low + out.shape[0], :]
+        low += out.shape[0]
 
 
 def chunk_rows(rows):
@@ -102,14 +101,14 @@
     return [step] * (CHUNKS - 1) + [rows - step * (CHUNKS - 1)]
 
 
-def compose(ctl_conv, ctl_hint, ctl_in, ctl_zero0, ctl_zero1, depth):
+def compose(order, ctl_conv, ctl_hint, ctl_in, ctl_zero0, ctl_zero1, depth):
     chans = ctl_conv.shape[3]
     wide = 3 * main_of(chans) + 2 * LANES
     rows = depth // 2 + 3 * (chans // 2)
-    shapes = [(size, wide) for size in chunk_rows(rows)] * 2
-    sources = (ctl_conv, ctl_hint, ctl_in, ctl_zero0, ctl_zero1)
+    shapes = [(size, wide) for size in chunk_rows(rows)]
+    sources = [far(array) for array in (ctl_conv, ctl_hint, ctl_in, ctl_zero0, ctl_zero1)]
     return pl.pallas_call(
-        compose_kernel,
+        functools.partial(compose_kernel, order=order),
         in_specs=[pl.BlockSpec(memory_space=pltpu.HBM)] * len(sources),
         out_shape=[jax.ShapeDtypeStruct(shape, jnp.bfloat16) for shape in shapes],
         scratch_shapes=[pltpu.VMEM(array.shape[1:], jnp.bfloat16) for array in sources]
@@ -120,8 +119,7 @@
             pltpu.SemaphoreType.DMA((len(sources),)),
         ],
         compiler_params=pltpu.CompilerParams(vmem_limit_bytes=20 * 1024 * 1024),
-        cost_estimate=cost(2 * 1216 * 320 * 1024 * 2),
-        name="compose",
+        cost_estimate=cost(2 * 608 * 320 * 1024 * 2),
     )(*sources)
 
 
@@ -160,6 +158,34 @@
         cost_estimate=cost(2 * 2880 * 320 * 256),
         name="arrange",
     )(unet_conv)
+
+
+def edges_kernel(last_ref, first_ref, lat_ref, next_out, last_out):
+    rows = lat_ref.shape[1]
+    cols, width = last_ref.shape[2:]
+    for out, hint_ref, low in ((next_out, last_ref, rows - 2), (last_out, first_ref, 0)):
+        out[...] = jnp.zeros_like(out)
+        out[:, 0:cols, 0:width] = hint_ref[:, 0]
+        out[:, cols : cols + 2, :] = lat_ref[:, low : low + 2, :]
+
+
+def edges_call(hint, latent):
+    batch, rows, cols, width = hint.shape
+    out = jax.ShapeDtypeStruct((batch, cols + 8, latent.shape[2]), jnp.bfloat16)
+    return pl.pallas_call(
+        edges_kernel,
+        grid=(1,),
+        in_specs=[
+            pl.BlockSpec((batch, 1, cols, width), lambda i: (0, rows - 1, 0, 0)),
+            pl.BlockSpec((batch, 1, cols, width), lambda i: (0, 0, 0, 0)),
+            pl.BlockSpec(latent.shape, lambda i: (0, 0, 0)),
+        ],
+        out_specs=[pl.BlockSpec(out.shape, lambda i: (0, 0, 0))] * 2,
+        out_shape=[out, out],
+        compiler_params=params(8),
+        cost_estimate=cost(1 << 20),
+        name="edges",
+    )(far(hint), far(hint), far(latent))
 
 
 def stem_kernel(
@@ -175,9 +201,8 @@
     _, _, double = weights.shape
     half = double // 2
     chans = unet_ref.shape[3]
-    _, rows, cols, width = hint_ref.shape
+    _, _, _, width = hint_ref.shape
     flat = lat_ref.shape[2]
-    bits = LCH.bit_length() - 1
 
     @pl.when(step == 0)
     def _():
@@ -195,6 +220,24 @@
         chosen = ((row & (LCH - 1)) == (col & (LCH - 1))) & (col >= 0) & (col < 9 * LCH)
         pick[...] = jnp.where(chosen, 1.0, 0.0).astype(jnp.bfloat16)
 
+    for i in range(hint_ref.shape[0]):
+        b = hint_ref.shape[0] * step + i
+        stem_request(
+            i, b, slot_of(cond_ref[b, 0], nets), lat_ref, hint_ref,
+            top_ref, bot_ref, u_ref, h_ref, a_ref, sums_ref, gain_ref,
+            weights, grid_in.at[i], spread_rows.at[i], pick, gains,
+        )
+
+
+def stem_request(
+    i, b, slot, lat_ref, hint_ref, top_ref, bot_ref, u_ref, h_ref, a_ref, sums_ref, gain_ref,
+    weights, grid_in, spread_rows, pick, gains,
+):
+    _, rows, cols, width = hint_ref.shape
+    flat = lat_ref.shape[2]
+    half = weights.shape[2] // 2
+    bits = LCH.bit_length() - 1
+
     at_x = lax.broadcasted_iota(jnp.int32, (cols, flat), 0)
     of_x = lax.broadcasted_iota(jnp.int32, (cols, flat), 1) >> bits
     lat_rows = (
@@ -202,9 +245,9 @@
         + [(lat_ref, r) for r in range(rows)]
         + [(bot_ref, cols + r) for r in range(2)]
     )
-    for i, (ref, r) in enumerate(lat_rows):
-        line = ref[0, r : r + 1, :].astype(jnp.float32)
-        spread_rows[i * cols : (i + 1) * cols, :] = jnp.where(of_x == at_x, line, 0.0).astype(
+    for j, (ref, r) in enumerate(lat_rows):
+        line = ref[i, r : r + 1, :].astype(jnp.float32)
+        spread_rows[j * cols : (j + 1) * cols, :] = jnp.where(of_x == at_x, line, 0.0).astype(
             jnp.bfloat16
         )
     cells = jnp.dot(spread_rows[...], pick[...], preferred_element_type=jnp.float32)
@@ -223,24 +266,27 @@
         jnp.where(tap_y == 1, beside[cols : cols + total], beside[2 * cols :]),
     ).astype(jnp.bfloat16)
 
-    grid_in[0:cols, 0:width] = top_ref[0, 0:cols, 0:width]
-    grid_in[cols : total - cols, 0:width] = hint_ref[0].reshape(rows * cols, width)
-    grid_in[total - cols : total, 0:width] = bot_ref[0, 0:cols, 0:width]
+    grid_in[0:cols, 0:width] = top_ref[i, 0:cols, 0:width]
+    grid_in[cols : total - cols, 0:width] = hint_ref[i].reshape(rows * cols, width)
+    grid_in[total - cols : total, 0:width] = bot_ref[i, 0:cols, 0:width]
     grid_in[:, width:] = patches[:, width % LANES :]
-    a_ref[0] = grid_in[cols : total - cols, :]
-    slot = slot_of(cond_ref[step, 0], nets)
+    a_ref[b] = grid_in[cols : total - cols, :]
     out = jnp.dot(grid_in[...], weights[slot], preferred_element_type=jnp.float32).astype(
         jnp.bfloat16
     )
-    u_ref[0] = out[:, 0:half].reshape(rows + 2, cols, half)
-    h_ref[0] = out[:, half:].reshape(rows + 2, cols, half)
+    u_ref[b] = out[:, 0:half].reshape(rows + 2, cols, half)
+    h_ref[b] = out[:, half:].reshape(rows + 2, cols, half)
     own = out[cols : total - cols].astype(jnp.float32)
     first = jnp.sum(own, axis=0, keepdims=True)
     second = jnp.sum(own * own, axis=0, keepdims=True)
-    sums_ref[0] = jnp.concatenate(
+    sums_ref[i] = jnp.concatenate(
         [first[:, 0:half], second[:, 0:half], first[:, half:], second[:, half:]], axis=0
     )
-    gain_ref[0] = gains[pl.ds(slot, 1), :]
+    gain_ref[i] = gains[pl.ds(slot, 1), :]
+
+
+def far(array):
+    return pltpu.with_memory_space_constraint(array, pltpu.HBM)
 
 
 def whole(array, space=None):
@@ -250,9 +296,9 @@
     return pl.BlockSpec(array.shape, lambda b: zeros)
 
 
-def per_request(array):
+def per_request(array, each=1):
     rest = (0,) * (array.ndim - 1)
-    return pl.BlockSpec((1,) + tuple(array.shape[1:]), lambda b: (b,) + rest)
+    return pl.BlockSpec((each,) + tuple(array.shape[1:]), lambda b: (b,) + rest)
 
 
 def stem_call(cond_ids, latent, hint, top, bot, unet_in, stems, depth):
@@ -262,6 +308,7 @@
     half = up_to(chans, LANES)
     total = (rows + 2) * cols
     flat = latent.shape[2]
+    each = 4 if batch % 4 == 0 else 1
     outs = [
         jax.ShapeDtypeStruct((batch, rows + 2, cols, half), jnp.bfloat16),
         jax.ShapeDtypeStruct((batch, rows + 2, cols, half), jnp.bfloat16),
@@ -272,22 +319,22 @@
     blocked = [latent, hint, top, bot]
     return pl.pallas_call(
         functools.partial(stem_kernel, nets=nets),
-        grid=(batch,),
+        grid=(batch // each,),
         in_specs=[whole(cond_ids, pltpu.SMEM)]
-        + [per_request(array) for array in blocked]
+        + [per_request(array, each) for array in blocked]
         + [whole(unet_in)]
         + [whole(array) for array in stems],
-        out_specs=[per_request(array) for array in outs],
+        out_specs=[held()] * 3 + [per_request(array, each) for array in outs[3:]],
         out_shape=outs,
         scratch_shapes=[
             pltpu.VMEM((nets, depth, 2 * half), jnp.bfloat16),
-            pltpu.VMEM((total, depth), jnp.bfloat16),
+            pltpu.VMEM((each, total, depth), jnp.bfloat16),
             pltpu.VMEM((depth, chans), jnp.float32),
-            pltpu.VMEM(((rows + 4) * cols, flat), jnp.bfloat16),
+            pltpu.VMEM((each, (rows + 4) * cols, flat), jnp.bfloat16),
             pltpu.VMEM((flat, LANES), jnp.bfloat16),
             pltpu.VMEM((up_to(nets, 8), half), jnp.float32),
         ],
-        compiler_params=params(14),
+        compiler_params=params(26),
         cost_estimate=cost(2 * batch * total * 256 * 896),
         name="stem",
     )(cond_ids, *blocked, unet_in, *stems)
@@ -329,7 +376,8 @@
     lhs[:, 3 * main + LANES :] = rest[2 * cols : 2 * cols + inner].astype(jnp.bfloat16)
 
 
-def spread(product, cols):
+def spread(columns, weight, product, cols, finish):
+    product = jnp.dot(columns, weight, preferred_element_type=jnp.float32)
     inner = product.shape[0]
     main = product.shape[1] // 4
     place = lax.broadcasted_iota(jnp.int32, (inner, 1), 0) % cols
@@ -350,37 +398,38 @@
     low = product[:, 3 * main : 3 * main + LANES]
     high = product[:, 3 * main + LANES :]
     tail = after(low) + pltpu.roll(low, LANES // 2, 1) + before(high)
-    return jnp.concatenate([head, tail], axis=1)
+    finish(0, inner, jnp.concatenate([head, tail], axis=1))
 
 
 def unet_kernel(
-    sums_ref, more_ref, gain_ref, pair_ref, next_ref, weight_ref, out_ref,
-    scale, shift, even, odd, *, count, group, chans,
+    sums_ref, more_ref, gain_ref, u_ref, weight_ref, out_ref,
+    scale, shift, even, odd, product, *, count, group, chans,
 ):
     step = pl.program_id(0)
     batch = sums_ref.shape[0]
-    _, total_rows, cols, lanes = pair_ref.shape
+    _, total_rows, cols, lanes = u_ref.shape
     rows = total_rows - 2
-    inner = rows * cols
-
-    def make(values, b, target):
-        values = values.reshape(total_rows * cols, lanes)
+
+    def make(b, target):
+        values = u_ref[b].reshape(total_rows * cols, lanes)
         normed_columns(values, scale[pl.ds(b, 1), :], shift[pl.ds(b, 1), :], target, rows, cols)
 
     def conv(columns, i):
-        product = jnp.dot(columns[...], weight_ref[...], preferred_element_type=jnp.float32)
-        own = pair_ref[i, 1 : 1 + rows].reshape(inner, lanes).astype(jnp.float32)
-        out_ref[i] = spread(product, cols) + own
+        def finish(at, size, values):
+            own = u_ref[2 * step + i, 1 : 1 + rows].reshape(size, lanes).astype(jnp.float32)
+            out_ref[2 * step + i, at : at + size] = (values + own).astype(out_ref.dtype)
+
+        spread(columns[...], weight_ref[...], product.at[i], cols, finish)
 
     @pl.when(step == 0)
     def _():
         gain = jnp.pad(gain_ref[...].astype(jnp.float32), ((0, 0), (0, lanes - chans)))
         group_affine(sums_ref, more_ref, 0, gain, count, group, chans, scale, shift)
-        make(pair_ref[0], 0, even)
-
-    make(pair_ref[1], 2 * step + 1, odd)
+        make(0, even)
+
+    make(2 * step + 1, odd)
     conv(even, 0)
-    make(next_ref[0], jnp.minimum(2 * step + 2, batch - 1), even)
+    make(jnp.minimum(2 * step + 2, batch - 1), even)
     conv(odd, 1)
 
 
@@ -389,49 +438,45 @@
     return pl.BlockSpec((2,) + tuple(array.shape[1:]), lambda b: (b,) + rest)
 
 
-def next_up(array):
-    rest = (0,) * (array.ndim - 1)
-    last = array.shape[0] - 1
-    return pl.BlockSpec(
-        (1,) + tuple(array.shape[1:]), lambda b: (jnp.minimum(2 * b + 2, last),) + rest
-    )
+def held():
+    return pl.BlockSpec(memory_space=pltpu.VMEM)
 
 
 def unet_call(sums, more, gain, unet_first, weight, count, group, chans):
     batch, total_rows, cols, lanes = unet_first.shape
     inner = (total_rows - 2) * cols
     depth = weight.shape[0]
-    out = jax.ShapeDtypeStruct((batch, inner, lanes), jnp.float32)
+    out = jax.ShapeDtypeStruct((batch, inner, lanes), jnp.bfloat16)
     return pl.pallas_call(
         functools.partial(unet_kernel, count=count, group=group, chans=chans),
         grid=(batch // 2,),
-        in_specs=[whole(sums), whole(more), whole(gain)]
-        + [in_pairs(unet_first), next_up(unet_first), whole(weight)],
-        out_specs=in_pairs(out),
+        in_specs=[whole(sums), whole(more), whole(gain), held(), held()],
+        out_specs=held(),
         scratch_shapes=[
             pltpu.VMEM((batch, lanes), jnp.float32),
             pltpu.VMEM((batch, lanes), jnp.float32),
             pltpu.VMEM((inner, depth), jnp.bfloat16),
             pltpu.VMEM((inner, depth), jnp.bfloat16),
+            pltpu.VMEM((2, 8, depth), jnp.float32),
         ],
         out_shape=out,
         compiler_params=params(24),
         cost_estimate=cost(2 * batch * inner * 1024 * 1024),
         name="unet_conv",
-    )(sums, more, gain, unet_first, unet_first, weight)
+    )(sums, more, gain, unet_first, weight)
 
 
 def control_kernel(
-    cond_ref, valid_ref, scale_ref, sums_ref, more_ref, gain_ref, pair_ref, next_ref, a_ref,
+    cond_ref, valid_ref, scale_ref, sums_ref, more_ref, gain_ref, h_ref, a_ref,
     u_ref, base_ref, *rest, nets, count, group, chans,
 ):
     pieces = rest[: 2 * CHUNKS * nets]
-    skip0_ref, skip1_ref, scale, shift, even, odd, weights, heads, sems = rest[
+    skip0_ref, skip1_ref, scale, shift, even, odd, product, weights, heads, here, sems = rest[
         2 * CHUNKS * nets :
     ]
     step = pl.program_id(0)
     batch = sums_ref.shape[0]
-    _, total_rows, cols, lanes = pair_ref.shape
+    _, total_rows, cols, lanes = h_ref.shape
     rows = total_rows - 2
     inner = rows * cols
     main = main_of(chans)
@@ -453,69 +498,103 @@
                     3 * main + dy * tail + begin - main,
                 )
 
-    def copies(flip):
+    def copies(n, flip):
         made = []
+        for order in range(2):
+            bound = 0
+            chunks = []
+            for piece in pieces[CHUNKS * (2 * n + order) : CHUNKS * (2 * n + order + 1)]:
+                chunks.append((bound, bound + piece.shape[0], piece))
+                bound += piece.shape[0]
+            for first, size, target, at, to in segments(n, order ^ flip):
+                for low, high, piece in chunks:
+                    start, stop = max(first, low), min(first + size, high)
+                    if start < stop:
+                        made.append(
+                            (
+                                piece.at[
+                                    pl.ds(start - low, stop - start), pl.ds(0, target.shape[2])
+                                ],
+                                target.at[at, pl.ds(to + start - first, stop - start), :],
+                            )
+                        )
+        return [pltpu.make_async_copy(s, t, sems.at[n, i]) for i, (s, t) in enumerate(made)]
+
+    side = lax.axis_index("rep") & 1
+
+    def for_net(n, act):
+        for flip in range(2):
+
+            @pl.when(side == flip)
+            def _():
+                for copy in copies(n, flip):
+                    act(copy)
+
+    def need(n):
+        @pl.when(here[n] == 0)
+        def _():
+            for_net(n, lambda copy: copy.wait())
+            here[n] = 1
+
+    def soon(n):
+        first, second = (slot_of(cond_ref[i, 0], nets) for i in range(2))
+        return (first == n) | (second == n)
+
+    def need_slot(slot):
         for n in range(nets):
-            for order in range(2):
-                bound = 0
-                chunks = []
-                for piece in pieces[CHUNKS * (2 * n + order) : CHUNKS * (2 * n + order + 1)]:
-                    chunks.append((bound, bound + piece.shape[0], piece))
-                    bound += piece.shape[0]
-                for first, size, target, at, to in segments(n, order ^ flip):
-                    for low, high, piece in chunks:
-                        start, stop = max(first, low), min(first + size, high)
-                        if start < stop:
-                            made.append(
-                                (
-                                    piece.at[
-                                        pl.ds(start - low, stop - start),
-                                        pl.ds(0, target.shape[2]),
-                                    ],
-                                    target.at[at, pl.ds(to + start - first, stop - start), :],
-                                )
-                            )
-        return [pltpu.make_async_copy(s, t, sems.at[i]) for i, (s, t) in enumerate(made)]
-
-    def for_side(act):
-        for flip in range(2):
-
-            @pl.when((lax.axis_index("rep") & 1) == flip)
-            def _():
-                for copy in copies(flip):
-                    act(copy)
-
-    def make(values, b, target):
-        values = values.reshape(total_rows * cols, lanes)
+            pl.when(slot == n)(functools.partial(need, n))
+
+    def make(b, target):
+        values = h_ref[b].reshape(total_rows * cols, lanes)
         normed_columns(values, scale[pl.ds(b, 1), :], shift[pl.ds(b, 1), :], target, rows, cols)
 
     def conv(columns, i):
         b = 2 * step + i
         slot = slot_of(cond_ref[b, 0], nets)
         live = scale_ref[b] * valid_ref[b].astype(jnp.float32)
-        heads_out = jnp.dot(a_ref[i], heads[slot], preferred_element_type=jnp.float32)
-        own = u_ref[i, 1 : 1 + rows].reshape(inner, lanes).astype(jnp.float32)
+        heads_out = jnp.dot(a_ref[b], heads[slot], preferred_element_type=jnp.float32)
+        own = u_ref[b, 1 : 1 + rows].reshape(inner, lanes).astype(jnp.float32)
         first = own + live * heads_out[:, 0:lanes]
         skip0_ref[i] = first[:, 0:chans].astype(jnp.bfloat16)
-        product = jnp.dot(columns[...], weights[slot], preferred_element_type=jnp.float32)
-        second = base_ref[i] + live * (spread(product, cols) + heads_out[:, lanes:])
-        skip1_ref[i] = second[:, 0:chans].astype(jnp.bfloat16)
+
+        def finish(at, size, values):
+            values = values + heads_out[at : at + size, lanes:]
+            second = base_ref[b, at : at + size].astype(jnp.float32) + live * values
+            skip1_ref[i, at : at + size] = second[:, 0:chans].astype(jnp.bfloat16)
+
+        spread(columns[...], weights[slot], product.at[i], cols, finish)
 
     @pl.when(step == 0)
     def _():
-        for_side(lambda copy: copy.start())
+        for n in range(nets):
+            here[n] = 0
+            pl.when(soon(n))(functools.partial(for_net, n, lambda copy: copy.start()))
         for n in range(nets):
             weights[n, 3 * chans :, :] = jnp.zeros(
                 (weights.shape[1] - 3 * chans, weights.shape[2]), jnp.bfloat16
             )
         group_affine(sums_ref, more_ref, 1, gain_ref[:, 0, :], count, group, chans, scale, shift)
-        make(pair_ref[0], 0, even)
-        for_side(lambda copy: copy.wait())
-
-    make(pair_ref[1], 2 * step + 1, odd)
+        make(0, even)
+
+    for i in range(2):
+        need_slot(slot_of(cond_ref[2 * step + i, 0], nets))
+
+    @pl.when(step == 0)
+    def _():
+        for n in range(nets):
+            pl.when(jnp.logical_not(soon(n)))(
+                functools.partial(for_net, n, lambda copy: copy.start())
+            )
+
+    make(2 * step + 1, odd)
     conv(even, 0)
-    make(next_ref[0], jnp.minimum(2 * step + 2, batch - 1), even)
+    make(jnp.minimum(2 * step + 2, batch - 1), even)
     conv(odd, 1)
+
+    @pl.when(step == pl.num_programs(0) - 1)
+    def _():
+        for n in range(nets):
+            need(n)
 
 
 def control_call(
@@ -525,6 +604,7 @@
     batch, total_rows, cols, lanes = control_first.shape
     inner = (total_rows - 2) * cols
     nets = len(pieces) // (2 * CHUNKS)
+    pieces = [far(piece) for piece in pieces]
     width = pieces[0].shape[1]
     depth = grids.shape[2]
     out = jax.ShapeDtypeStruct((batch, inner, chans), jnp.bfloat16)
@@ -533,8 +613,7 @@
         grid=(batch // 2,),
         in_specs=[whole(array, pltpu.SMEM) for array in (cond_ids, valid, cond_scale)]
         + [whole(sums), whole(more), whole(gains)]
-        + [in_pairs(control_first), next_up(control_first)]
-        + [in_pairs(array) for array in (grids, unet_first, base)]
+        + [held()] * 4
         + [whole(array, pl.ANY) for array in pieces],
         out_specs=[in_pairs(out), in_pairs(out)],
         scratch_shapes=[
@@ -542,16 +621,18 @@
             pltpu.VMEM((batch, lanes), jnp.float32),
             pltpu.VMEM((inner, width), jnp.bfloat16),
             pltpu.VMEM((inner, width), jnp.bfloat16),
+            pltpu.VMEM((2, 8, width), jnp.float32),
             pltpu.VMEM((nets, width, width), jnp.bfloat16),
             pltpu.VMEM((nets, depth, 2 * lanes), jnp.bfloat16),
-            pltpu.SemaphoreType.DMA((16 * CHUNKS * nets,)),
+            pltpu.SMEM((nets,), jnp.int32),
+            pltpu.SemaphoreType.DMA((nets, 16 * CHUNKS)),
         ],
         out_shape=[out, out],
         compiler_params=params(24 + 3 * nets),
         cost_estimate=cost(2 * batch * inner * 1024 * 1280),
         name="control_conv",
     )(
-        cond_ids, valid, cond_scale, sums, more, gains, control_first, control_first, grids,
+        cond_ids, valid, cond_scale, sums, more, gains, control_first, grids,
         unet_first, base, *pieces,
     )
 
@@ -592,16 +673,15 @@
     for got in far:
         stems += got + across(got)
 
-    def edge(hint_row, lat_rows):
-        wide = jnp.pad(hint_row, ((0, 0), (0, 0), (0, flat - hint_row.shape[2])))
-        return jnp.pad(jnp.concatenate([wide, lat_rows], axis=1), ((0, 0), (0, 6), (0, 0)))
-
     down = [(r, r + 1) for r in range(reps - 1)]
     up = [(r + 1, r) for r in range(reps - 1)]
-    (top,) = moved([edge(hint[:, rows - 1], latent[:, rows - 2 :])], "rep", down)
-    (bot,) = moved([edge(hint[:, 0], latent[:, :2])], "rep", up)
-
-    own = compose(ctl_conv, ctl_hint, ctl_in, ctl_zero0, ctl_zero1, depth)
+    to_next, to_last = edges_call(hint, latent)
+    (top,) = moved([to_next], "rep", down)
+    (bot,) = moved([to_last], "rep", up)
+
+    own = []
+    for order in range(2):
+        own += compose(order, ctl_conv, ctl_hint, ctl_in, ctl_zero0, ctl_zero1, depth)
     away = [along_net(own[:CHUNKS], s) for s in range(1, nets // 2)]
     pieces = list(own) + across(own)
     for got in away:

time: 133 us -> 127 us (0.955)
  local copies, waits for them, and re-layouts: 17.1 us -> 11.8 us
  waiting for transfers between devices: 36.9 us -> 35.4 us
    pallas_call x2 -> x4, Pallas kernels: 12.8 us -> 17.2 us  [the longest x1 7.74 us: stem_call(): pl.pallas_call(functools.partial(stem_kernel, nets=nets), grid=(batch //...]
    pallas_call x1, Pallas kernels: 25.9 us -> 21.5 us  [control_call(): pl.pallas_call(functools.partial(control_kernel, nets=nets, count=count,...]
    unnamed x63 -> x91, local copies, waits for them, and re-layouts: 13.7 us -> 11.8 us
    ppermute x32, waiting for transfers between devices: 36.9 us -> 35.4 us  [moved(): got.append(lax.ppermute(array, axis, pairs))]
    pad x2 -> x0, local copies, waits for them, and re-layouts: 1.47 us -> none  [edge(): jnp.pad(jnp.concatenate([wide, lat_rows], axis=1), ((0, 0), (0, 6), (0, 0)))]
  transfers between devices with their start and end apart: 32 -> 32, of which waited for: 8 -> 9; matrix products, arithmetic and copies ran while one was open for 3% -> 1% of each run, Pallas kernels for 19% -> 23%
where the time goes in v2:
time: 127 us
  Pallas kernels  50.9 us (40%)
  waiting for transfers between devices  35.4 us (28%)
  starting transfers between devices  27.5 us (22%)
  local copies, waits for them, and re-layouts  11.8 us (9%)
    ppermute x32, waiting for transfers between devices, moved(): got.append(lax.ppermute(array, axis, pairs))  35.4 us
    ppermute x32, starting transfers between devices, moved(): got.append(lax.ppermute(array, axis, pairs))  27.5 us
    pallas_call x1, Pallas kernels, control_call(): pl.pallas_call(functools.partial(control_kernel, nets=nets, count=count,...  21.5 us
    unnamed x91, local copies, waits for them, and re-layouts  11.8 us
    pallas_call x1, Pallas kernels, unet_call(): pl.pallas_call(functools.partial(unet_kernel, count=count, group=group, c...  11.4 us
    pallas_call x1, Pallas kernels, stem_call(): pl.pallas_call(functools.partial(stem_kernel, nets=nets), grid=(batch //...  7.74 us
    pallas_call x2, Pallas kernels, compose(): pl.pallas_call(functools.partial(compose_kernel, order=order), in_specs=[...  7.61 us
  transfers between devices with their start and end apart: 32, of which 9 were waited for; matrix products, arithmetic and copies ran while one was open for 1% of the time, Pallas kernels for 23%

profile of v2, /device:TPU:0, one launch (start us, length us, event | category | flops | bytes accessed | tf_op | source)
XLA Modules:
  0.0 126.9 jit_solution(5615919989421888892)
XLA Ops:
  0.7 3.0 %collective-permute-start.7 = (bf16[1,192,320]{2,1,0:T(8,128)(2,1)}, bf16[1,192,320]{2,1,0:T(8,128)(2,1)S(1)}, u32[]{:S(2)}, u32[]{:S(2)}) collective-permute-start(bf16[1,192,320]{2,1,0:T(8,128)(2,1)} %refs_1_.3), channel_id=1, source_target_pairs={{0,16},{8,24},{16,0},{24,8},{1,17},{9,25},{17,1},{25,9},{2,18},{10... | collective-permute-start | bytes 368648 | tf_op jit(solution)/shard_map/ppermute | solution.py:657
  3.7 1.9 %edges.1 = (bf16[8,72,256]{2,1,0:T(8,128)(2,1)}, bf16[8,72,256]{2,1,0:T(8,128)(2,1)}) custom-call(bf16[8,8,64,192]{3,2,1,0:T(8,128)(2,1)} %hint_ref.1, bf16[8,8,64,192]{3,2,1,0:T(8,128)(2,1)} %hint_ref.1, bf16[8,8,256]{2,1,0:T(8,128)(2,1)} %lat_ref.3), custom_call_target="tpu_custom_call" | custom-call | flops 1048576 | bytes 1048576 | tf_op jit(solution)/shard_map/edges/pallas_call | solution.py:175
  5.6 4.3 %collective-permute-start = (bf16[8,72,256]{2,1,0:T(8,128)(2,1)}, bf16[8,72,256]{2,1,0:T(8,128)(2,1)}, u32[]{:S(2)}, u32[]{:S(2)}) collective-permute-start(bf16[8,72,256]{2,1,0:T(8,128)(2,1)} %get-tuple-element.17), channel_id=1, source_target_pairs={{0,1},{1,2},{2,3},{3,4},{4,5},{5,6},{6,7},{8,9},{9,10},{10,11},{11... | collective-permute-start | bytes 884744 | tf_op jit(solution)/shard_map/ppermute | solution.py:657
  9.9 1.3 %collective-permute-start.1 = (bf16[8,72,256]{2,1,0:T(8,128)(2,1)}, bf16[8,72,256]{2,1,0:T(8,128)(2,1)}, u32[]{:S(2)}, u32[]{:S(2)}) collective-permute-start(bf16[8,72,256]{2,1,0:T(8,128)(2,1)} %get-tuple-element.18), channel_id=1, source_target_pairs={{1,0},{2,1},{3,2},{4,3},{5,4},{6,5},{7,6},{9,8},{10,9},{11,10},{12... | collective-permute-start | bytes 884744 | tf_op jit(solution)/shard_map/ppermute | solution.py:657
  11.8 1.2 collective-permute-done.3.rest_4_
  13.5 1.5 %collective-permute-start.6 = (bf16[1,320]{1,0:T(2,128)(2,1)S(1)}, bf16[1,320]{1,0:T(2,128)(2,1)S(1)}, u32[]{:S(2)}, u32[]{:S(2)}) collective-permute-start(bf16[1,320]{1,0:T(2,128)(2,1)S(1)} %copy-done.19), channel_id=1, source_target_pairs={{0,16},{8,24},{16,0},{24,8},{1,17},{9,25},{17,1},{25,9},{2,18},{10... | collective-permute-start | bytes 1928 | tf_op jit(solution)/shard_map/ppermute | solution.py:657
  15.0 2.1 %collective-permute-done.6.rest_7_ = bf16[1,320]{1,0:T(2,128)(2,1)S(1)} collective-permute-done((bf16[1,320]{1,0:T(2,128)(2,1)S(1)}, bf16[1,320]{1,0:T(2,128)(2,1)S(1)}, u32[]{:S(2)}, u32[]{:S(2)}) %collective-permute-start.6) | collective-permute-done | bytes 672 | tf_op jit(solution)/shard_map/ppermute | solution.py:657
  19.0 3.8 %shard_map.150 = (bf16[208,1024]{1,0:T(8,128)(2,1)S(1)}, bf16[208,1024]{1,0:T(8,128)(2,1)S(1)}, bf16[192,1024]{1,0:T(8,128)(2,1)}) custom-call(bf16[1,3,3,320,320]{4,3,2,1,0:T(8,128)(2,1)} %refs_0_.3, bf16[1,192,320]{2,1,0:T(8,128)(2,1)} %refs_1_.3, bf16[1,3,3,4,320]{4,3,2,1,0:T(4,128)(2,1)} %refs_2_.3, bf16[1,320,320]{2,1,0:T(8,128)(2,1)} %refs_3_.3, ...), custom_call_target="tpu_custom_call" | custom-call | flops 796917760 | bytes 1048576 | tf_op jit(solution)/shard_map/pallas_call | solution.py:110
  23.2 3.8 %shard_map.149 = (bf16[208,1024]{1,0:T(8,128)(2,1)S(1)}, bf16[208,1024]{1,0:T(8,128)(2,1)S(1)}, bf16[192,1024]{1,0:T(8,128)(2,1)}) custom-call(bf16[1,3,3,320,320]{4,3,2,1,0:T(8,128)(2,1)} %refs_0_.3, bf16[1,192,320]{2,1,0:T(8,128)(2,1)} %refs_1_.3, bf16[1,3,3,4,320]{4,3,2,1,0:T(4,128)(2,1)} %refs_2_.3, bf16[1,320,320]{2,1,0:T(8,128)(2,1)} %refs_3_.3, ...), custom_call_target="tpu_custom_call" | custom-call | flops 796917760 | bytes 1048576 | tf_op jit(solution)/shard_map/pallas_call | solution.py:110
  28.7 1.5 %collective-permute-start.22 = (bf16[192,1024]{1,0:T(8,128)(2,1)}, bf16[192,1024]{1,0:T(8,128)(2,1)}, u32[]{:S(2)}, u32[]{:S(2)}) collective-permute-start(bf16[192,1024]{1,0:T(8,128)(2,1)} %get-tuple-element.26.rest_2_), channel_id=1, source_target_pairs={{0,16},{8,24},{16,0},{24,8},{1,17},{9,25},{17,1},{25,9},{2,18},{10... | collective-permute-start | bytes 1179656 | tf_op jit(solution)/shard_map/ppermute | solution.py:657
  31.7 1.1 copy-done.9
  38.2 7.7 %stem.1 = (bf16[8,10,64,384]{3,2,1,0:T(8,128)(2,1)S(1)}, bf16[8,10,64,384]{3,2,1,0:T(8,128)(2,1)S(1)}, bf16[8,512,256]{2,1,0:T(8,128)(2,1)S(1)}, f32[8,4,384]{2,1,0:T(4,128)S(1)}, f32[8,1,384]{2,1,0:T(1,128)S(1)}) custom-call(s32[8,1]{1,0:T(8,128)S(1)} %copy.17.cond_ref, bf16[8,8,256]{2,1,0:T(8,128)(2,1)S(1)} %copy-done.2, ...), custom_call_target="tpu_custom_call" | custom-call | flops 2348810240 | bytes 1048576 | tf_op jit(solution)/shard_map/stem/pallas_call | solution.py:320
  45.9 2.7 %collective-permute-start.11 = (f32[8,4,384]{2,1,0:T(4,128)S(1)}, f32[8,4,384]{2,1,0:T(4,128)S(1)}, u32[]{:S(2)}, u32[]{:S(2)}) collective-permute-start(f32[8,4,384]{2,1,0:T(4,128)S(1)} %get-tuple-element.19), channel_id=1, source_target_pairs={{0,1},{1,0},{2,3},{3,2},{4,5},{5,4},{6,7},{7,6},{8,9},{9,8},{10,11... | collective-permute-start | bytes 147464 | tf_op jit(solution)/shard_map/ppermute | solution.py:657
  48.8 2.2 %collective-permute-done.11 = f32[8,4,384]{2,1,0:T(4,128)S(1)} collective-permute-done((f32[8,4,384]{2,1,0:T(4,128)S(1)}, f32[8,4,384]{2,1,0:T(4,128)S(1)}, u32[]{:S(2)}, u32[]{:S(2)}) %collective-permute-start.11) | collective-permute-done | bytes 49184 | tf_op jit(solution)/shard_map/ppermute | solution.py:657
  51.0 2.0 %collective-permute-start.12 = (f32[8,4,384]{2,1,0:T(4,128)S(1)}, f32[8,4,384]{2,1,0:T(4,128)S(1)}, u32[]{:S(2)}, u32[]{:S(2)}) collective-permute-start(f32[8,4,384]{2,1,0:T(4,128)S(1)} %add.6), channel_id=1, source_target_pairs={{0,2},{1,3},{2,0},{3,1},{4,6},{5,7},{6,4},{7,5},{8,10},{9,11},{10,... | collective-permute-start | bytes 147464 | tf_op jit(solution)/shard_map/ppermute | solution.py:657
  53.6 1.5 %collective-permute-start.21 = (bf16[208,1024]{1,0:T(8,128)(2,1)S(1)}, bf16[208,1024]{1,0:T(8,128)(2,1)S(1)}, u32[]{:S(2)}, u32[]{:S(2)}) collective-permute-start(bf16[208,1024]{1,0:T(8,128)(2,1)S(1)} %copy-done.7), channel_id=1, source_target_pairs={{0,16},{8,24},{16,0},{24,8},{1,17},{9,25},{17,1},{25,9},{2,18},{10... | collective-permute-start | bytes 1277960 | tf_op jit(solution)/shard_map/ppermute | solution.py:657
  55.7 10.0 %collective-permute-done.20.rest_12_ = bf16[208,1024]{1,0:T(8,128)(2,1)S(1)} collective-permute-done((bf16[208,1024]{1,0:T(8,128)(2,1)S(1)}, bf16[208,1024]{1,0:T(8,128)(2,1)S(1)}, u32[]{:S(2)}, u32[]{:S(2)}) %collective-permute-start.20) | collective-permute-done | bytes 426016 | tf_op jit(solution)/shard_map/ppermute | solution.py:657
  66.4 6.8 %collective-permute-done.21.rest_13_ = bf16[208,1024]{1,0:T(8,128)(2,1)S(1)} collective-permute-done((bf16[208,1024]{1,0:T(8,128)(2,1)S(1)}, bf16[208,1024]{1,0:T(8,128)(2,1)S(1)}, u32[]{:S(2)}, u32[]{:S(2)}) %collective-permute-start.21) | collective-permute-done | bytes 426016 | tf_op jit(solution)/shard_map/ppermute | solution.py:657
  73.9 1.4 %collective-permute-start.25 = (bf16[192,1024]{1,0:T(8,128)(2,1)}, bf16[192,1024]{1,0:T(8,128)(2,1)S(1)}, u32[]{:S(2)}, u32[]{:S(2)}) collective-permute-start(bf16[192,1024]{1,0:T(8,128)(2,1)} %collective-permute-done.22.rest_14_), channel_id=1, source_target_pairs={{0,1},{1,0},{2,3},{3,2},{4,5},{5,4},{6,7},{7,6},{8,9},{9,8},{10,11... | collective-permute-start | bytes 1179656 | tf_op jit(solution)/shard_map/ppermute | solution.py:657
  75.4 2.7 %collective-permute-start.13 = (f32[8,4,384]{2,1,0:T(4,128)S(1)}, f32[8,4,384]{2,1,0:T(4,128)S(1)}, u32[]{:S(2)}, u32[]{:S(2)}) collective-permute-start(f32[8,4,384]{2,1,0:T(4,128)S(1)} %add.7.sums_ref), channel_id=1, source_target_pairs={{0,4},{1,5},{2,6},{3,7},{4,0},{5,1},{6,2},{7,3},{8,12},{9,13},{10,... | collective-permute-start | bytes 147464 | tf_op jit(solution)/shard_map/ppermute | solution.py:657
  78.9 2.1 %collective-permute-done.13.more_ref = f32[8,4,384]{2,1,0:T(4,128)S(1)} collective-permute-done((f32[8,4,384]{2,1,0:T(4,128)S(1)}, f32[8,4,384]{2,1,0:T(4,128)S(1)}, u32[]{:S(2)}, u32[]{:S(2)}) %collective-permute-start.13) | collective-permute-done | bytes 49184 | tf_op jit(solution)/shard_map/ppermute | solution.py:657
  81.6 10.3 %collective-permute-done.25.rest_17_ = bf16[192,1024]{1,0:T(8,128)(2,1)S(1)} collective-permute-done((bf16[192,1024]{1,0:T(8,128)(2,1)}, bf16[192,1024]{1,0:T(8,128)(2,1)S(1)}, u32[]{:S(2)}, u32[]{:S(2)}) %collective-permute-start.25) | collective-permute-done | bytes 393248 | tf_op jit(solution)/shard_map/ppermute | solution.py:657
  92.5 11.4 %unet_conv.1.base_ref = bf16[8,512,384]{2,1,0:T(8,128)(2,1)S(1)} custom-call(f32[8,4,384]{2,1,0:T(4,128)S(1)} %add.7.sums_ref, f32[8,4,384]{2,1,0:T(4,128)S(1)} %collective-permute-done.13.more_ref, bf16[1,320]{1,0:T(2,128)(2,1)S(1)} %broadcast_in_dim.3.gain_ref, bf16[8,10,64,384]{3,2,1,0:T(8,128)(2,1)S(1)} %get-tuple-element.23.u_ref, ...), custom_call_target="tpu_custom_call" | custom-call | flops 8589934592 | bytes 1048576 | tf_op jit(solution)/shard_map/unet_conv/pallas_call | solution.py:450
  105.3 21.5 %control_conv.1 = (bf16[8,512,320]{2,1,0:T(8,128)(2,1)}, bf16[8,512,320]{2,1,0:T(8,128)(2,1)}) custom-call(s32[8,1]{1,0:T(8,128)S(1)} %copy.17.cond_ref, s32[8]{0:T(128)S(1)} %copy-done.27, f32[8]{0:T(128)S(1)} %copy-done.28, f32[8,4,384]{2,1,0:T(4,128)S(1)} %add.7.sums_ref, f32[8,4,384]{2,1,0:T(4,128)S(1)} %collective-permute-done.13.more_ref, ...), custom_call_target="tpu_custom_call" | custom-call | flops 10737418240 | bytes 1048576 | tf_op jit(solution)/shard_map/control_conv/pallas_call | solution.py:611
  (141 shorter events, 17.9 us)
Async XLA Ops:
  0.7 18.1 %collective-permute-start.7 = (bf16[1,192,320]{2,1,0:T(8,128)(2,1)}, bf16[1,192,320]{2,1,0:T(8,128)(2,1)S(1)}, u32[]{:S(2)}, u32[]{:S(2)}) collective-permute-start(bf16[1,192,320]{2,1,0:T(8,128)(2,1)} %refs_1_.3), channel_id=1, source_target_pairs={{0,16},{8,24},{16,0},{24,8},{1,17},{9,25},{17,1},{25,9},{2,18},{10... | collective-permute-start | bytes 368648 | tf_op jit(solution)/shard_map/ppermute | solution.py:657
  5.6 26.0 %collective-permute-start = (bf16[8,72,256]{2,1,0:T(8,128)(2,1)}, bf16[8,72,256]{2,1,0:T(8,128)(2,1)}, u32[]{:S(2)}, u32[]{:S(2)}) collective-permute-start(bf16[8,72,256]{2,1,0:T(8,128)(2,1)} %get-tuple-element.17), channel_id=1, source_target_pairs={{0,1},{1,2},{2,3},{3,4},{4,5},{5,6},{6,7},{8,9},{9,10},{10,11},{11... | collective-permute-start | bytes 884744 | tf_op jit(solution)/shard_map/ppermute | solution.py:657
  9.9 21.7 %collective-permute-start.1 = (bf16[8,72,256]{2,1,0:T(8,128)(2,1)}, bf16[8,72,256]{2,1,0:T(8,128)(2,1)}, u32[]{:S(2)}, u32[]{:S(2)}) collective-permute-start(bf16[8,72,256]{2,1,0:T(8,128)(2,1)} %get-tuple-element.18), channel_id=1, source_target_pairs={{1,0},{2,1},{3,2},{4,3},{5,4},{6,5},{7,6},{9,8},{10,9},{11,10},{12... | collective-permute-start | bytes 884744 | tf_op jit(solution)/shard_map/ppermute | solution.py:657
  11.2 7.3 %collective-permute-start.5 = (bf16[1,3,3,4,320]{4,3,2,1,0:T(4,128)(2,1)S(1)}, bf16[1,3,3,4,320]{4,3,2,1,0:T(4,128)(2,1)S(1)}, u32[]{:S(2)}, u32[]{:S(2)}) collective-permute-start(bf16[1,3,3,4,320]{4,3,2,1,0:T(4,128)(2,1)S(1)} %copy-done.17), channel_id=1, source_target_pairs={{0,16},{8,24},{16,0},{24,8},{1,17},{9,25},{17,1},{25,9},{2,18},{10... | collective-permute-start | bytes 69128 | tf_op jit(solution)/shard_map/ppermute | solution.py:657
  18.5 9.6 %collective-permute-start.4 = (bf16[1,192,320]{2,1,0:T(8,128)(2,1)S(1)}, bf16[1,192,320]{2,1,0:T(8,128)(2,1)S(1)}, u32[]{:S(2)}, u32[]{:S(2)}) collective-permute-start(bf16[1,192,320]{2,1,0:T(8,128)(2,1)S(1)} %copy-done.8), channel_id=1, source_target_pairs={{0,8},{8,0},{16,24},{24,16},{1,9},{9,1},{17,25},{25,17},{2,10},{10... | collective-permute-start | bytes 368648 | tf_op jit(solution)/shard_map/ppermute | solution.py:657
  18.8 11.4 %collective-permute-start.10 = (bf16[1,192,320]{2,1,0:T(8,128)(2,1)S(1)}, bf16[1,192,320]{2,1,0:T(8,128)(2,1)S(1)}, u32[]{:S(2)}, u32[]{:S(2)}) collective-permute-start(bf16[1,192,320]{2,1,0:T(8,128)(2,1)S(1)} %collective-permute-done.7.rest_8_), channel_id=1, source_target_pairs={{0,8},{8,0},{16,24},{24,16},{1,9},{9,1},{17,25},{25,17},{2,10},{10... | collective-permute-start | bytes 368648 | tf_op jit(solution)/shard_map/ppermute | solution.py:657
  27.8 25.2 %collective-permute-start.19 = (bf16[192,1024]{1,0:T(8,128)(2,1)}, bf16[192,1024]{1,0:T(8,128)(2,1)}, u32[]{:S(2)}, u32[]{:S(2)}) collective-permute-start(bf16[192,1024]{1,0:T(8,128)(2,1)} %get-tuple-element.29.rest_5_), channel_id=1, source_target_pairs={{0,8},{8,0},{16,24},{24,16},{1,9},{9,1},{17,25},{25,17},{2,10},{10... | collective-permute-start | bytes 1179656 | tf_op jit(solution)/shard_map/ppermute | solution.py:657
  28.7 24.9 %collective-permute-start.22 = (bf16[192,1024]{1,0:T(8,128)(2,1)}, bf16[192,1024]{1,0:T(8,128)(2,1)}, u32[]{:S(2)}, u32[]{:S(2)}) collective-permute-start(bf16[192,1024]{1,0:T(8,128)(2,1)} %get-tuple-element.26.rest_2_), channel_id=1, source_target_pairs={{0,16},{8,24},{16,0},{24,8},{1,17},{9,25},{17,1},{25,9},{2,18},{10... | collective-permute-start | bytes 1179656 | tf_op jit(solution)/shard_map/ppermute | solution.py:657
  30.8 24.2 %collective-permute-start.16 = (bf16[192,1024]{1,0:T(8,128)(2,1)}, bf16[192,1024]{1,0:T(8,128)(2,1)}, u32[]{:S(2)}, u32[]{:S(2)}) collective-permute-start(bf16[192,1024]{1,0:T(8,128)(2,1)} %get-tuple-element.26.rest_2_), channel_id=1, source_target_pairs={{0,8},{8,0},{16,24},{24,16},{1,9},{9,1},{17,25},{25,17},{2,10},{10... | collective-permute-start | bytes 1179656 | tf_op jit(solution)/shard_map/ppermute | solution.py:657
  48.6 7.0 %collective-permute-start.17 = (bf16[208,1024]{1,0:T(8,128)(2,1)S(1)}, bf16[208,1024]{1,0:T(8,128)(2,1)S(1)}, u32[]{:S(2)}, u32[]{:S(2)}) collective-permute-start(bf16[208,1024]{1,0:T(8,128)(2,1)S(1)} %get-tuple-element.27.rest_3_), channel_id=1, source_target_pairs={{0,8},{8,0},{16,24},{24,16},{1,9},{9,1},{17,25},{25,17},{2,10},{10... | collective-permute-start | bytes 1277960 | tf_op jit(solution)/shard_map/ppermute | solution.py:657
  53.1 12.7 %collective-permute-start.20 = (bf16[208,1024]{1,0:T(8,128)(2,1)S(1)}, bf16[208,1024]{1,0:T(8,128)(2,1)S(1)}, u32[]{:S(2)}, u32[]{:S(2)}) collective-permute-start(bf16[208,1024]{1,0:T(8,128)(2,1)S(1)} %get-tuple-element.24.rest_0_), channel_id=1, source_target_pairs={{0,16},{8,24},{16,0},{24,8},{1,17},{9,25},{17,1},{25,9},{2,18},{10... | collective-permute-start | bytes 1277960 | tf_op jit(solution)/shard_map/ppermute | solution.py:657
  53.6 19.6 %collective-permute-start.21 = (bf16[208,1024]{1,0:T(8,128)(2,1)S(1)}, bf16[208,1024]{1,0:T(8,128)(2,1)S(1)}, u32[]{:S(2)}, u32[]{:S(2)}) collective-permute-start(bf16[208,1024]{1,0:T(8,128)(2,1)S(1)} %copy-done.7), channel_id=1, source_target_pairs={{0,16},{8,24},{16,0},{24,8},{1,17},{9,25},{17,1},{25,9},{2,18},{10... | collective-permute-start | bytes 1277960 | tf_op jit(solution)/shard_map/ppermute | solution.py:657
  55.1 18.8 %collective-permute-start.18 = (bf16[208,1024]{1,0:T(8,128)(2,1)S(1)}, bf16[208,1024]{1,0:T(8,128)(2,1)S(1)}, u32[]{:S(2)}, u32[]{:S(2)}) collective-permute-start(bf16[208,1024]{1,0:T(8,128)(2,1)S(1)} %get-tuple-element.28.rest_4_), channel_id=1, source_target_pairs={{0,8},{8,0},{16,24},{24,16},{1,9},{9,1},{17,25},{25,17},{2,10},{10... | collective-permute-start | bytes 1277960 | tf_op jit(solution)/shard_map/ppermute | solution.py:657
  55.2 18.7 %collective-permute-start.14 = (bf16[208,1024]{1,0:T(8,128)(2,1)S(1)}, bf16[208,1024]{1,0:T(8,128)(2,1)S(1)}, u32[]{:S(2)}, u32[]{:S(2)}) collective-permute-start(bf16[208,1024]{1,0:T(8,128)(2,1)S(1)} %get-tuple-element.24.rest_0_), channel_id=1, source_target_pairs={{0,8},{8,0},{16,24},{24,16},{1,9},{9,1},{17,25},{25,17},{2,10},{10... | collective-permute-start | bytes 1277960 | tf_op jit(solution)/shard_map/ppermute | solution.py:657
  55.6 19.8 %collective-permute-start.15 = (bf16[208,1024]{1,0:T(8,128)(2,1)S(1)}, bf16[208,1024]{1,0:T(8,128)(2,1)S(1)}, u32[]{:S(2)}, u32[]{:S(2)}) collective-permute-start(bf16[208,1024]{1,0:T(8,128)(2,1)S(1)} %copy-done.7), channel_id=1, source_target_pairs={{0,8},{8,0},{16,24},{24,16},{1,9},{9,1},{17,25},{25,17},{2,10},{10... | collective-permute-start | bytes 1277960 | tf_op jit(solution)/shard_map/ppermute | solution.py:657
  65.7 26.1 %collective-permute-start.23 = (bf16[208,1024]{1,0:T(8,128)(2,1)S(1)}, bf16[208,1024]{1,0:T(8,128)(2,1)S(1)}, u32[]{:S(2)}, u32[]{:S(2)}) collective-permute-start(bf16[208,1024]{1,0:T(8,128)(2,1)S(1)} %collective-permute-done.20.rest_12_), channel_id=1, source_target_pairs={{0,1},{1,0},{2,3},{3,2},{4,5},{5,4},{6,7},{7,6},{8,9},{9,8},{10,11... | collective-permute-start | bytes 1277960 | tf_op jit(solution)/shard_map/ppermute | solution.py:657
  73.2 19.1 %collective-permute-start.24 = (bf16[208,1024]{1,0:T(8,128)(2,1)S(1)}, bf16[208,1024]{1,0:T(8,128)(2,1)S(1)}, u32[]{:S(2)}, u32[]{:S(2)}) collective-permute-start(bf16[208,1024]{1,0:T(8,128)(2,1)S(1)} %collective-permute-done.21.rest_13_), channel_id=1, source_target_pairs={{0,1},{1,0},{2,3},{3,2},{4,5},{5,4},{6,7},{7,6},{8,9},{9,8},{10,11... | collective-permute-start | bytes 1277960 | tf_op jit(solution)/shard_map/ppermute | solution.py:657
  73.9 7.2 %collective-permute-start.28 = (bf16[192,1024]{1,0:T(8,128)(2,1)}, bf16[192,1024]{1,0:T(8,128)(2,1)S(1)}, u32[]{:S(2)}, u32[]{:S(2)}) collective-permute-start(bf16[192,1024]{1,0:T(8,128)(2,1)} %collective-permute-done.22.rest_14_), channel_id=1, source_target_pairs={{0,8},{8,0},{16,24},{24,16},{1,9},{9,1},{17,25},{25,17},{2,10},{10... | collective-permute-start | bytes 1179656 | tf_op jit(solution)/shard_map/ppermute | solution.py:657
  73.9 17.9 %collective-permute-start.25 = (bf16[192,1024]{1,0:T(8,128)(2,1)}, bf16[192,1024]{1,0:T(8,128)(2,1)S(1)}, u32[]{:S(2)}, u32[]{:S(2)}) collective-permute-start(bf16[192,1024]{1,0:T(8,128)(2,1)} %collective-permute-done.22.rest_14_), channel_id=1, source_target_pairs={{0,1},{1,0},{2,3},{3,2},{4,5},{5,4},{6,7},{7,6},{8,9},{9,8},{10,11... | collective-permute-start | bytes 1179656 | tf_op jit(solution)/shard_map/ppermute | solution.py:657
  81.0 22.9 %collective-permute-start.26 = (bf16[208,1024]{1,0:T(8,128)(2,1)S(1)}, bf16[208,1024]{1,0:T(8,128)(2,1)S(1)}, u32[]{:S(2)}, u32[]{:S(2)}) collective-permute-start(bf16[208,1024]{1,0:T(8,128)(2,1)S(1)} %collective-permute-done.20.rest_12_), channel_id=1, source_target_pairs={{0,8},{8,0},{16,24},{24,16},{1,9},{9,1},{17,25},{25,17},{2,10},{10... | collective-permute-start | bytes 1277960 | tf_op jit(solution)/shard_map/ppermute | solution.py:657
  81.0 22.9 %collective-permute-start.27 = (bf16[208,1024]{1,0:T(8,128)(2,1)S(1)}, bf16[208,1024]{1,0:T(8,128)(2,1)S(1)}, u32[]{:S(2)}, u32[]{:S(2)}) collective-permute-start(bf16[208,1024]{1,0:T(8,128)(2,1)S(1)} %collective-permute-done.21.rest_13_), channel_id=1, source_target_pairs={{0,8},{8,0},{16,24},{24,16},{1,9},{9,1},{17,25},{25,17},{2,10},{10... | collective-permute-start | bytes 1277960 | tf_op jit(solution)/shard_map/ppermute | solution.py:657
  91.8 12.1 %collective-permute-start.31 = (bf16[192,1024]{1,0:T(8,128)(2,1)S(1)}, bf16[192,1024]{1,0:T(8,128)(2,1)S(1)}, u32[]{:S(2)}, u32[]{:S(2)}) collective-permute-start(bf16[192,1024]{1,0:T(8,128)(2,1)S(1)} %collective-permute-done.25.rest_17_), channel_id=1, source_target_pairs={{0,8},{8,0},{16,24},{24,16},{1,9},{9,1},{17,25},{25,17},{2,10},{10... | collective-permute-start | bytes 1179656 | tf_op jit(solution)/shard_map/ppermute | solution.py:657
  91.9 12.1 %collective-permute-start.29 = (bf16[208,1024]{1,0:T(8,128)(2,1)S(1)}, bf16[208,1024]{1,0:T(8,128)(2,1)S(1)}, u32[]{:S(2)}, u32[]{:S(2)}) collective-permute-start(bf16[208,1024]{1,0:T(8,128)(2,1)S(1)} %collective-permute-done.23.rest_15_), channel_id=1, source_target_pairs={{0,8},{8,0},{16,24},{24,16},{1,9},{9,1},{17,25},{25,17},{2,10},{10... | collective-permute-start | bytes 1277960 | tf_op jit(solution)/shard_map/ppermute | solution.py:657
  92.4 11.6 %collective-permute-start.30 = (bf16[208,1024]{1,0:T(8,128)(2,1)S(1)}, bf16[208,1024]{1,0:T(8,128)(2,1)S(1)}, u32[]{:S(2)}, u32[]{:S(2)}) collective-permute-start(bf16[208,1024]{1,0:T(8,128)(2,1)S(1)} %collective-permute-done.24.rest_16_), channel_id=1, source_target_pairs={{0,8},{8,0},{16,24},{24,16},{1,9},{9,1},{17,25},{25,17},{2,10},{10... | collective-permute-start | bytes 1277960 | tf_op jit(solution)/shard_map/ppermute | solution.py:657
  (53 other events, 695.5 us)

commit v3 on v2

--- a/solution.py
+++ b/solution.py
@@ -12,7 +12,7 @@
 GROUPS = 32
 LANES = 128
 EPS = 1e-05
-CHUNKS = 3
+CHUNKS = 2
 
 
 def up_to(value, step):
@@ -684,8 +684,9 @@
         own += compose(order, ctl_conv, ctl_hint, ctl_in, ctl_zero0, ctl_zero1, depth)
     away = [along_net(own[:CHUNKS], s) for s in range(1, nets // 2)]
     pieces = list(own) + across(own)
-    for got in away:
-        full = got + beside(got)
+    for s, got in enumerate(away):
+        late = along_net(own[-1:], s + 1)
+        full = got + beside(got[: CHUNKS - 1]) + late
         pieces += full + across(full)
 
     unet_first, control_first, grids, sums, gains = stem_call(

time: 127 us -> 118 us (0.929)
  waiting for transfers between devices: 35.4 us -> 27.2 us
    ppermute x32 -> x26, waiting for transfers between devices: 35.4 us -> 27.2 us  [moved(): got.append(lax.ppermute(array, axis, pairs))]
    ppermute x32 -> x26, starting transfers between devices: 27.5 us -> 26.4 us  [moved(): got.append(lax.ppermute(array, axis, pairs))]
    unnamed x91 -> x75, local copies, waits for them, and re-layouts: 11.8 us -> 11.7 us
  transfers between devices with their start and end apart: 32 -> 26, of which waited for: 9 -> 7; matrix products, arithmetic and copies ran while one was open for 1% -> 1% of each run, Pallas kernels for 23% -> 25%
where the time goes in v3:
time: 118 us; the launch traced here: 117 us
  Pallas kernels  49.7 us (42%)
  waiting for transfers between devices  27.2 us (23%)
  starting transfers between devices  26.4 us (22%)
  local copies, waits for them, and re-layouts  12.4 us (11%)
    ppermute x26, waiting for transfers between devices, moved(): got.append(lax.ppermute(array, axis, pairs))  27.2 us
    ppermute x26, starting transfers between devices, moved(): got.append(lax.ppermute(array, axis, pairs))  26.4 us
    pallas_call x1, Pallas kernels, control_call(): pl.pallas_call(functools.partial(control_kernel, nets=nets, count=count,...  20.4 us
    unnamed x75, local copies, waits for them, and re-layouts  11.7 us
    pallas_call x1, Pallas kernels, unet_call(): pl.pallas_call(functools.partial(unet_kernel, count=count, group=group, c...  11.4 us
    pallas_call x1, Pallas kernels, stem_call(): pl.pallas_call(functools.partial(stem_kernel, nets=nets), grid=(batch //...  7.89 us
    pallas_call x2, Pallas kernels, compose(): pl.pallas_call(functools.partial(compose_kernel, order=order), in_specs=[...  6.81 us
    pallas_call x1, Pallas kernels, edges_call(): pl.pallas_call(edges_kernel, grid=(1,), in_specs=[pl.BlockSpec((batch, 1,...  2.41 us
  transfers between devices with their start and end apart: 26, of which 7 were waited for; matrix products, arithmetic and copies ran while one was open for 1% of the time, Pallas kernels for 25%

profile of v3, /device:TPU:0, one launch (start us, length us, event | category | flops | bytes accessed | tf_op | source)
XLA Modules:
  0.0 116.8 jit_solution(17877465453199003719)
XLA Ops:
  0.6 3.0 %collective-permute-start.6 = (bf16[1,320]{1,0:T(2,128)(2,1)}, bf16[1,320]{1,0:T(2,128)(2,1)S(1)}, u32[]{:S(2)}, u32[]{:S(2)}) collective-permute-start(bf16[1,320]{1,0:T(2,128)(2,1)} %rest_1_.1), channel_id=1, source_target_pairs={{0,16},{8,24},{16,0},{24,8},{1,17},{9,25},{17,1},{25,9},{2,18},{10... | collective-permute-start | bytes 1928 | tf_op jit(solution)/shard_map/ppermute | solution.py:657
  4.2 1.7 %collective-permute-start.7 = (bf16[1,192,320]{2,1,0:T(8,128)(2,1)}, bf16[1,192,320]{2,1,0:T(8,128)(2,1)}, u32[]{:S(2)}, u32[]{:S(2)}) collective-permute-start(bf16[1,192,320]{2,1,0:T(8,128)(2,1)} %refs_1_.3), channel_id=1, source_target_pairs={{0,16},{8,24},{16,0},{24,8},{1,17},{9,25},{17,1},{25,9},{2,18},{10... | collective-permute-start | bytes 368648 | tf_op jit(solution)/shard_map/ppermute | solution.py:657
  5.9 3.0 %shard_map.150 = (bf16[304,1024]{1,0:T(8,128)(2,1)S(1)}, bf16[304,1024]{1,0:T(8,128)(2,1)S(1)}) custom-call(bf16[1,3,3,320,320]{4,3,2,1,0:T(8,128)(2,1)} %refs_0_.3, bf16[1,192,320]{2,1,0:T(8,128)(2,1)} %refs_1_.3, bf16[1,3,3,4,320]{4,3,2,1,0:T(4,128)(2,1)} %refs_2_.3, bf16[1,320,320]{2,1,0:T(8,128)(2,1)} %refs_3_.3, bf16[1,320,320]{2,1,0:T(8,128)(2,1)} %refs_4_.3), custom_call_target="tpu_custom_call" | custom-call | flops 796917760 | bytes 1048576 | tf_op jit(solution)/shard_map/pallas_call | solution.py:110
  9.0 2.4 %edges.1 = (bf16[8,72,256]{2,1,0:T(8,128)(2,1)}, bf16[8,72,256]{2,1,0:T(8,128)(2,1)}) custom-call(bf16[8,8,64,192]{3,2,1,0:T(8,128)(2,1)} %hint_ref.1, bf16[8,8,64,192]{3,2,1,0:T(8,128)(2,1)} %hint_ref.1, bf16[8,8,256]{2,1,0:T(8,128)(2,1)} %lat_ref.3), custom_call_target="tpu_custom_call" | custom-call | flops 1048576 | bytes 1048576 | tf_op jit(solution)/shard_map/edges/pallas_call | solution.py:175
  11.4 4.2 %collective-permute-start = (bf16[8,72,256]{2,1,0:T(8,128)(2,1)}, bf16[8,72,256]{2,1,0:T(8,128)(2,1)}, u32[]{:S(2)}, u32[]{:S(2)}) collective-permute-start(bf16[8,72,256]{2,1,0:T(8,128)(2,1)} %get-tuple-element.15), channel_id=1, source_target_pairs={{0,1},{1,2},{2,3},{3,4},{4,5},{5,6},{6,7},{8,9},{9,10},{10,11},{11... | collective-permute-start | bytes 884744 | tf_op jit(solution)/shard_map/ppermute | solution.py:657
  15.6 1.3 %collective-permute-start.1 = (bf16[8,72,256]{2,1,0:T(8,128)(2,1)}, bf16[8,72,256]{2,1,0:T(8,128)(2,1)}, u32[]{:S(2)}, u32[]{:S(2)}) collective-permute-start(bf16[8,72,256]{2,1,0:T(8,128)(2,1)} %get-tuple-element.16), channel_id=1, source_target_pairs={{1,0},{2,1},{3,2},{4,3},{5,4},{6,5},{7,6},{9,8},{10,9},{11,10},{12... | collective-permute-start | bytes 884744 | tf_op jit(solution)/shard_map/ppermute | solution.py:657
  17.3 3.8 %shard_map.149 = (bf16[304,1024]{1,0:T(8,128)(2,1)}, bf16[304,1024]{1,0:T(8,128)(2,1)S(1)}) custom-call(bf16[1,3,3,320,320]{4,3,2,1,0:T(8,128)(2,1)} %refs_0_.3, bf16[1,192,320]{2,1,0:T(8,128)(2,1)} %refs_1_.3, bf16[1,3,3,4,320]{4,3,2,1,0:T(4,128)(2,1)} %refs_2_.3, bf16[1,320,320]{2,1,0:T(8,128)(2,1)} %refs_3_.3, bf16[1,320,320]{2,1,0:T(8,128)(2,1)} %refs_4_.3), custom_call_target="tpu_custom_call" | custom-call | flops 796917760 | bytes 1048576 | tf_op jit(solution)/shard_map/pallas_call | solution.py:110
  23.4 1.5 %collective-permute-start.18 = (bf16[304,1024]{1,0:T(8,128)(2,1)}, bf16[304,1024]{1,0:T(8,128)(2,1)}, u32[]{:S(2)}, u32[]{:S(2)}) collective-permute-start(bf16[304,1024]{1,0:T(8,128)(2,1)} %get-tuple-element.22.rest_0_), channel_id=1, source_target_pairs={{0,16},{8,24},{16,0},{24,8},{1,17},{9,25},{17,1},{25,9},{2,18},{10... | collective-permute-start | bytes 1867784 | tf_op jit(solution)/shard_map/ppermute | solution.py:657
  24.9 1.4 %collective-permute-done.4.rest_5_ = bf16[1,192,320]{2,1,0:T(8,128)(2,1)S(1)} collective-permute-done((bf16[1,192,320]{2,1,0:T(8,128)(2,1)S(1)}, bf16[1,192,320]{2,1,0:T(8,128)(2,1)S(1)}, u32[]{:S(2)}, u32[]{:S(2)}) %collective-permute-start.4) | collective-permute-done | bytes 122912 | tf_op jit(solution)/shard_map/ppermute | solution.py:657
  27.8 0.8 collective-permute-done.10.rest_11_
  28.7 0.9 copy-done.9
  35.2 7.9 %stem.1 = (bf16[8,10,64,384]{3,2,1,0:T(8,128)(2,1)S(1)}, bf16[8,10,64,384]{3,2,1,0:T(8,128)(2,1)S(1)}, bf16[8,512,256]{2,1,0:T(8,128)(2,1)S(1)}, f32[8,4,384]{2,1,0:T(4,128)S(1)}, f32[8,1,384]{2,1,0:T(1,128)S(1)}) custom-call(s32[8,1]{1,0:T(8,128)S(1)} %copy.17.cond_ref, bf16[8,8,256]{2,1,0:T(8,128)(2,1)S(1)} %copy-done.2, ...), custom_call_target="tpu_custom_call" | custom-call | flops 2348810240 | bytes 1048576 | tf_op jit(solution)/shard_map/stem/pallas_call | solution.py:320
  43.1 2.7 %collective-permute-start.11 = (f32[8,4,384]{2,1,0:T(4,128)S(1)}, f32[8,4,384]{2,1,0:T(4,128)S(1)}, u32[]{:S(2)}, u32[]{:S(2)}) collective-permute-start(f32[8,4,384]{2,1,0:T(4,128)S(1)} %get-tuple-element.17), channel_id=1, source_target_pairs={{0,1},{1,0},{2,3},{3,2},{4,5},{5,4},{6,7},{7,6},{8,9},{9,8},{10,11... | collective-permute-start | bytes 147464 | tf_op jit(solution)/shard_map/ppermute | solution.py:657
  45.8 2.2 %collective-permute-done.11 = f32[8,4,384]{2,1,0:T(4,128)S(1)} collective-permute-done((f32[8,4,384]{2,1,0:T(4,128)S(1)}, f32[8,4,384]{2,1,0:T(4,128)S(1)}, u32[]{:S(2)}, u32[]{:S(2)}) %collective-permute-start.11) | collective-permute-done | bytes 49184 | tf_op jit(solution)/shard_map/ppermute | solution.py:657
  48.1 2.5 %collective-permute-start.12 = (f32[8,4,384]{2,1,0:T(4,128)S(1)}, f32[8,4,384]{2,1,0:T(4,128)S(1)}, u32[]{:S(2)}, u32[]{:S(2)}) collective-permute-start(f32[8,4,384]{2,1,0:T(4,128)S(1)} %add.6), channel_id=1, source_target_pairs={{0,2},{1,3},{2,0},{3,1},{4,6},{5,7},{6,4},{7,5},{8,10},{9,11},{10,... | collective-permute-start | bytes 147464 | tf_op jit(solution)/shard_map/ppermute | solution.py:657
  50.6 2.1 %collective-permute-done.12 = f32[8,4,384]{2,1,0:T(4,128)S(1)} collective-permute-done((f32[8,4,384]{2,1,0:T(4,128)S(1)}, f32[8,4,384]{2,1,0:T(4,128)S(1)}, u32[]{:S(2)}, u32[]{:S(2)}) %collective-permute-start.12) | collective-permute-done | bytes 49184 | tf_op jit(solution)/shard_map/ppermute | solution.py:657
  52.7 3.1 %collective-permute-start.13 = (f32[8,4,384]{2,1,0:T(4,128)S(1)}, f32[8,4,384]{2,1,0:T(4,128)S(1)}, u32[]{:S(2)}, u32[]{:S(2)}) collective-permute-start(f32[8,4,384]{2,1,0:T(4,128)S(1)} %add.7.sums_ref), channel_id=1, source_target_pairs={{0,4},{1,5},{2,6},{3,7},{4,0},{5,1},{6,2},{7,3},{8,12},{9,13},{10,... | collective-permute-start | bytes 147464 | tf_op jit(solution)/shard_map/ppermute | solution.py:657
  55.8 1.5 %collective-permute-start.21 = (bf16[304,1024]{1,0:T(8,128)(2,1)S(1)}, bf16[304,1024]{1,0:T(8,128)(2,1)S(1)}, u32[]{:S(2)}, u32[]{:S(2)}) collective-permute-start(bf16[304,1024]{1,0:T(8,128)(2,1)S(1)} %get-tuple-element.25.rest_3_), channel_id=1, source_target_pairs={{0,16},{8,24},{16,0},{24,8},{1,17},{9,25},{17,1},{25,9},{2,18},{10... | collective-permute-start | bytes 1867784 | tf_op jit(solution)/shard_map/ppermute | solution.py:657
  57.9 1.6 %collective-permute-start.19 = (bf16[304,1024]{1,0:T(8,128)(2,1)S(1)}, bf16[304,1024]{1,0:T(8,128)(2,1)S(1)}, u32[]{:S(2)}, u32[]{:S(2)}) collective-permute-start(bf16[304,1024]{1,0:T(8,128)(2,1)S(1)} %copy-done.6), channel_id=1, source_target_pairs={{0,16},{8,24},{16,0},{24,8},{1,17},{9,25},{17,1},{25,9},{2,18},{10... | collective-permute-start | bytes 1867784 | tf_op jit(solution)/shard_map/ppermute | solution.py:657
  59.4 1.0 collective-permute-start.20
  61.9 10.8 %collective-permute-done.21.rest_11_ = bf16[304,1024]{1,0:T(8,128)(2,1)S(1)} collective-permute-done((bf16[304,1024]{1,0:T(8,128)(2,1)S(1)}, bf16[304,1024]{1,0:T(8,128)(2,1)S(1)}, u32[]{:S(2)}, u32[]{:S(2)}) %collective-permute-start.21) | collective-permute-done | bytes 622624 | tf_op jit(solution)/shard_map/ppermute | solution.py:657
  73.3 9.2 %collective-permute-done.19.rest_9_ = bf16[304,1024]{1,0:T(8,128)(2,1)S(1)} collective-permute-done((bf16[304,1024]{1,0:T(8,128)(2,1)S(1)}, bf16[304,1024]{1,0:T(8,128)(2,1)S(1)}, u32[]{:S(2)}, u32[]{:S(2)}) %collective-permute-start.19) | collective-permute-done | bytes 622624 | tf_op jit(solution)/shard_map/ppermute | solution.py:657
  83.1 11.4 %unet_conv.1.base_ref = bf16[8,512,384]{2,1,0:T(8,128)(2,1)S(1)} custom-call(f32[8,4,384]{2,1,0:T(4,128)S(1)} %add.7.sums_ref, f32[8,4,384]{2,1,0:T(4,128)S(1)} %collective-permute-done.13.more_ref, bf16[1,320]{1,0:T(2,128)(2,1)S(1)} %broadcast_in_dim.3.gain_ref, bf16[8,10,64,384]{3,2,1,0:T(8,128)(2,1)S(1)} %get-tuple-element.21.u_ref, ...), custom_call_target="tpu_custom_call" | custom-call | flops 8589934592 | bytes 1048576 | tf_op jit(solution)/shard_map/unet_conv/pallas_call | solution.py:450
  96.3 20.4 %control_conv.1 = (bf16[8,512,320]{2,1,0:T(8,128)(2,1)}, bf16[8,512,320]{2,1,0:T(8,128)(2,1)}) custom-call(s32[8,1]{1,0:T(8,128)S(1)} %copy.17.cond_ref, s32[8]{0:T(128)S(1)} %copy-done.25, f32[8]{0:T(128)S(1)} %copy-done.26, f32[8,4,384]{2,1,0:T(4,128)S(1)} %add.7.sums_ref, f32[8,4,384]{2,1,0:T(4,128)S(1)} %collective-permute-done.13.more_ref, ...), custom_call_target="tpu_custom_call" | custom-call | flops 10737418240 | bytes 1048576 | tf_op jit(solution)/shard_map/control_conv/pallas_call | solution.py:611
  (113 shorter events, 15.3 us)
Async XLA Ops:
  0.6 5.3 %collective-permute-start.6 = (bf16[1,320]{1,0:T(2,128)(2,1)}, bf16[1,320]{1,0:T(2,128)(2,1)S(1)}, u32[]{:S(2)}, u32[]{:S(2)}) collective-permute-start(bf16[1,320]{1,0:T(2,128)(2,1)} %rest_1_.1), channel_id=1, source_target_pairs={{0,16},{8,24},{16,0},{24,8},{1,17},{9,25},{17,1},{25,9},{2,18},{10... | collective-permute-start | bytes 1928 | tf_op jit(solution)/shard_map/ppermute | solution.py:657
  3.7 7.8 %collective-permute-start.3 = (bf16[1,320]{1,0:T(2,128)(2,1)}, bf16[1,320]{1,0:T(2,128)(2,1)S(1)}, u32[]{:S(2)}, u32[]{:S(2)}) collective-permute-start(bf16[1,320]{1,0:T(2,128)(2,1)} %rest_1_.1), channel_id=1, source_target_pairs={{0,8},{8,0},{16,24},{24,16},{1,9},{9,1},{17,25},{25,17},{2,10},{10... | collective-permute-start | bytes 1928 | tf_op jit(solution)/shard_map/ppermute | solution.py:657
  3.7 13.3 %collective-permute-start.5 = (bf16[1,3,3,4,320]{4,3,2,1,0:T(4,128)(2,1)}, bf16[1,3,3,4,320]{4,3,2,1,0:T(4,128)(2,1)S(1)}, u32[]{:S(2)}, u32[]{:S(2)}) collective-permute-start(bf16[1,3,3,4,320]{4,3,2,1,0:T(4,128)(2,1)} %refs_2_.3), channel_id=1, source_target_pairs={{0,16},{8,24},{16,0},{24,8},{1,17},{9,25},{17,1},{25,9},{2,18},{10... | collective-permute-start | bytes 69128 | tf_op jit(solution)/shard_map/ppermute | solution.py:657
  3.8 18.1 %collective-permute-start.2 = (bf16[1,3,3,4,320]{4,3,2,1,0:T(4,128)(2,1)}, bf16[1,3,3,4,320]{4,3,2,1,0:T(4,128)(2,1)S(1)}, u32[]{:S(2)}, u32[]{:S(2)}) collective-permute-start(bf16[1,3,3,4,320]{4,3,2,1,0:T(4,128)(2,1)} %refs_2_.3), channel_id=1, source_target_pairs={{0,8},{8,0},{16,24},{24,16},{1,9},{9,1},{17,25},{25,17},{2,10},{10... | collective-permute-start | bytes 69128 | tf_op jit(solution)/shard_map/ppermute | solution.py:657
  4.2 20.7 %collective-permute-start.7 = (bf16[1,192,320]{2,1,0:T(8,128)(2,1)}, bf16[1,192,320]{2,1,0:T(8,128)(2,1)}, u32[]{:S(2)}, u32[]{:S(2)}) collective-permute-start(bf16[1,192,320]{2,1,0:T(8,128)(2,1)} %refs_1_.3), channel_id=1, source_target_pairs={{0,16},{8,24},{16,0},{24,8},{1,17},{9,25},{17,1},{25,9},{2,18},{10... | collective-permute-start | bytes 368648 | tf_op jit(solution)/shard_map/ppermute | solution.py:657
  5.9 9.7 %collective-permute-start.9 = (bf16[1,320]{1,0:T(2,128)(2,1)S(1)}, bf16[1,320]{1,0:T(2,128)(2,1)S(1)}, u32[]{:S(2)}, u32[]{:S(2)}) collective-permute-start(bf16[1,320]{1,0:T(2,128)(2,1)S(1)} %collective-permute-done.6.rest_7_), channel_id=1, source_target_pairs={{0,8},{8,0},{16,24},{24,16},{1,9},{9,1},{17,25},{25,17},{2,10},{10... | collective-permute-start | bytes 1928 | tf_op jit(solution)/shard_map/ppermute | solution.py:657
  11.4 17.2 %collective-permute-start = (bf16[8,72,256]{2,1,0:T(8,128)(2,1)}, bf16[8,72,256]{2,1,0:T(8,128)(2,1)}, u32[]{:S(2)}, u32[]{:S(2)}) collective-permute-start(bf16[8,72,256]{2,1,0:T(8,128)(2,1)} %get-tuple-element.15), channel_id=1, source_target_pairs={{0,1},{1,2},{2,3},{3,4},{4,5},{5,6},{6,7},{8,9},{9,10},{10,11},{11... | collective-permute-start | bytes 884744 | tf_op jit(solution)/shard_map/ppermute | solution.py:657
  15.6 13.0 %collective-permute-start.1 = (bf16[8,72,256]{2,1,0:T(8,128)(2,1)}, bf16[8,72,256]{2,1,0:T(8,128)(2,1)}, u32[]{:S(2)}, u32[]{:S(2)}) collective-permute-start(bf16[8,72,256]{2,1,0:T(8,128)(2,1)} %get-tuple-element.16), channel_id=1, source_target_pairs={{1,0},{2,1},{3,2},{4,3},{5,4},{6,5},{7,6},{9,8},{10,9},{11,10},{12... | collective-permute-start | bytes 884744 | tf_op jit(solution)/shard_map/ppermute | solution.py:657
  17.0 5.8 %collective-permute-start.8 = (bf16[1,3,3,4,320]{4,3,2,1,0:T(4,128)(2,1)S(1)}, bf16[1,3,3,4,320]{4,3,2,1,0:T(4,128)(2,1)S(1)}, u32[]{:S(2)}, u32[]{:S(2)}) collective-permute-start(bf16[1,3,3,4,320]{4,3,2,1,0:T(4,128)(2,1)S(1)} %collective-permute-done.5.rest_6_), channel_id=1, source_target_pairs={{0,8},{8,0},{16,24},{24,16},{1,9},{9,1},{17,25},{25,17},{2,10},{10... | collective-permute-start | bytes 69128 | tf_op jit(solution)/shard_map/ppermute | solution.py:657
  22.5 35.4 %collective-permute-start.16 = (bf16[304,1024]{1,0:T(8,128)(2,1)S(1)}, bf16[304,1024]{1,0:T(8,128)(2,1)}, u32[]{:S(2)}, u32[]{:S(2)}) collective-permute-start(bf16[304,1024]{1,0:T(8,128)(2,1)S(1)} %get-tuple-element.24.rest_2_), channel_id=1, source_target_pairs={{0,8},{8,0},{16,24},{24,16},{1,9},{9,1},{17,25},{25,17},{2,10},{10... | collective-permute-start | bytes 1867784 | tf_op jit(solution)/shard_map/ppermute | solution.py:657
  23.4 36.0 %collective-permute-start.18 = (bf16[304,1024]{1,0:T(8,128)(2,1)}, bf16[304,1024]{1,0:T(8,128)(2,1)}, u32[]{:S(2)}, u32[]{:S(2)}) collective-permute-start(bf16[304,1024]{1,0:T(8,128)(2,1)} %get-tuple-element.22.rest_0_), channel_id=1, source_target_pairs={{0,16},{8,24},{16,0},{24,8},{1,17},{9,25},{17,1},{25,9},{2,18},{10... | collective-permute-start | bytes 1867784 | tf_op jit(solution)/shard_map/ppermute | solution.py:657
  43.1 5.0 %collective-permute-start.11 = (f32[8,4,384]{2,1,0:T(4,128)S(1)}, f32[8,4,384]{2,1,0:T(4,128)S(1)}, u32[]{:S(2)}, u32[]{:S(2)}) collective-permute-start(f32[8,4,384]{2,1,0:T(4,128)S(1)} %get-tuple-element.17), channel_id=1, source_target_pairs={{0,1},{1,0},{2,3},{3,2},{4,5},{5,4},{6,7},{7,6},{8,9},{9,8},{10,11... | collective-permute-start | bytes 147464 | tf_op jit(solution)/shard_map/ppermute | solution.py:657
  48.1 4.6 %collective-permute-start.12 = (f32[8,4,384]{2,1,0:T(4,128)S(1)}, f32[8,4,384]{2,1,0:T(4,128)S(1)}, u32[]{:S(2)}, u32[]{:S(2)}) collective-permute-start(f32[8,4,384]{2,1,0:T(4,128)S(1)} %add.6), channel_id=1, source_target_pairs={{0,2},{1,3},{2,0},{3,1},{4,6},{5,7},{6,4},{7,5},{8,10},{9,11},{10,... | collective-permute-start | bytes 147464 | tf_op jit(solution)/shard_map/ppermute | solution.py:657
  52.7 5.2 %collective-permute-start.13 = (f32[8,4,384]{2,1,0:T(4,128)S(1)}, f32[8,4,384]{2,1,0:T(4,128)S(1)}, u32[]{:S(2)}, u32[]{:S(2)}) collective-permute-start(f32[8,4,384]{2,1,0:T(4,128)S(1)} %add.7.sums_ref), channel_id=1, source_target_pairs={{0,4},{1,5},{2,6},{3,7},{4,0},{5,1},{6,2},{7,3},{8,12},{9,13},{10,... | collective-permute-start | bytes 147464 | tf_op jit(solution)/shard_map/ppermute | solution.py:657
  55.8 16.9 %collective-permute-start.21 = (bf16[304,1024]{1,0:T(8,128)(2,1)S(1)}, bf16[304,1024]{1,0:T(8,128)(2,1)S(1)}, u32[]{:S(2)}, u32[]{:S(2)}) collective-permute-start(bf16[304,1024]{1,0:T(8,128)(2,1)S(1)} %get-tuple-element.25.rest_3_), channel_id=1, source_target_pairs={{0,16},{8,24},{16,0},{24,8},{1,17},{9,25},{17,1},{25,9},{2,18},{10... | collective-permute-start | bytes 1867784 | tf_op jit(solution)/shard_map/ppermute | solution.py:657
  57.3 15.4 %collective-permute-start.17 = (bf16[304,1024]{1,0:T(8,128)(2,1)S(1)}, bf16[304,1024]{1,0:T(8,128)(2,1)S(1)}, u32[]{:S(2)}, u32[]{:S(2)}) collective-permute-start(bf16[304,1024]{1,0:T(8,128)(2,1)S(1)} %get-tuple-element.25.rest_3_), channel_id=1, source_target_pairs={{0,8},{8,0},{16,24},{24,16},{1,9},{9,1},{17,25},{25,17},{2,10},{10... | collective-permute-start | bytes 1867784 | tf_op jit(solution)/shard_map/ppermute | solution.py:657
  57.9 15.4 %collective-permute-start.14 = (bf16[304,1024]{1,0:T(8,128)(2,1)}, bf16[304,1024]{1,0:T(8,128)(2,1)S(1)}, u32[]{:S(2)}, u32[]{:S(2)}) collective-permute-start(bf16[304,1024]{1,0:T(8,128)(2,1)} %get-tuple-element.22.rest_0_), channel_id=1, source_target_pairs={{0,8},{8,0},{16,24},{24,16},{1,9},{9,1},{17,25},{25,17},{2,10},{10... | collective-permute-start | bytes 1867784 | tf_op jit(solution)/shard_map/ppermute | solution.py:657
  57.9 24.7 %collective-permute-start.19 = (bf16[304,1024]{1,0:T(8,128)(2,1)S(1)}, bf16[304,1024]{1,0:T(8,128)(2,1)S(1)}, u32[]{:S(2)}, u32[]{:S(2)}) collective-permute-start(bf16[304,1024]{1,0:T(8,128)(2,1)S(1)} %copy-done.6), channel_id=1, source_target_pairs={{0,16},{8,24},{16,0},{24,8},{1,17},{9,25},{17,1},{25,9},{2,18},{10... | collective-permute-start | bytes 1867784 | tf_op jit(solution)/shard_map/ppermute | solution.py:657
  59.4 23.1 %collective-permute-start.20 = (bf16[304,1024]{1,0:T(8,128)(2,1)}, bf16[304,1024]{1,0:T(8,128)(2,1)S(1)}, u32[]{:S(2)}, u32[]{:S(2)}) collective-permute-start(bf16[304,1024]{1,0:T(8,128)(2,1)} %collective-permute-done.18.rest_8_), channel_id=1, source_target_pairs={{0,1},{1,0},{2,3},{3,2},{4,5},{5,4},{6,7},{7,6},{8,9},{9,8},{10,11... | collective-permute-start | bytes 1867784 | tf_op jit(solution)/shard_map/ppermute | solution.py:657
  72.7 21.8 %collective-permute-start.15 = (bf16[304,1024]{1,0:T(8,128)(2,1)S(1)}, bf16[304,1024]{1,0:T(8,128)(2,1)S(1)}, u32[]{:S(2)}, u32[]{:S(2)}) collective-permute-start(bf16[304,1024]{1,0:T(8,128)(2,1)S(1)} %copy-done.6), channel_id=1, source_target_pairs={{0,8},{8,0},{16,24},{24,16},{1,9},{9,1},{17,25},{25,17},{2,10},{10... | collective-permute-start | bytes 1867784 | tf_op jit(solution)/shard_map/ppermute | solution.py:657
  72.7 21.8 %collective-permute-start.22 = (bf16[304,1024]{1,0:T(8,128)(2,1)}, bf16[304,1024]{1,0:T(8,128)(2,1)S(1)}, u32[]{:S(2)}, u32[]{:S(2)}) collective-permute-start(bf16[304,1024]{1,0:T(8,128)(2,1)} %collective-permute-done.18.rest_8_), channel_id=1, source_target_pairs={{0,8},{8,0},{16,24},{24,16},{1,9},{9,1},{17,25},{25,17},{2,10},{10... | collective-permute-start | bytes 1867784 | tf_op jit(solution)/shard_map/ppermute | solution.py:657
  73.2 21.3 %collective-permute-start.25 = (bf16[304,1024]{1,0:T(8,128)(2,1)S(1)}, bf16[304,1024]{1,0:T(8,128)(2,1)S(1)}, u32[]{:S(2)}, u32[]{:S(2)}) collective-permute-start(bf16[304,1024]{1,0:T(8,128)(2,1)S(1)} %collective-permute-done.21.rest_11_), channel_id=1, source_target_pairs={{0,8},{8,0},{16,24},{24,16},{1,9},{9,1},{17,25},{25,17},{2,10},{10... | collective-permute-start | bytes 1867784 | tf_op jit(solution)/shard_map/ppermute | solution.py:657
  82.5 12.0 %collective-permute-start.23 = (bf16[304,1024]{1,0:T(8,128)(2,1)S(1)}, bf16[304,1024]{1,0:T(8,128)(2,1)S(1)}, u32[]{:S(2)}, u32[]{:S(2)}) collective-permute-start(bf16[304,1024]{1,0:T(8,128)(2,1)S(1)} %collective-permute-done.19.rest_9_), channel_id=1, source_target_pairs={{0,8},{8,0},{16,24},{24,16},{1,9},{9,1},{17,25},{25,17},{2,10},{10... | collective-permute-start | bytes 1867784 | tf_op jit(solution)/shard_map/ppermute | solution.py:657
  82.6 12.0 %collective-permute-start.24 = (bf16[304,1024]{1,0:T(8,128)(2,1)S(1)}, bf16[304,1024]{1,0:T(8,128)(2,1)S(1)}, u32[]{:S(2)}, u32[]{:S(2)}) collective-permute-start(bf16[304,1024]{1,0:T(8,128)(2,1)S(1)} %collective-permute-done.20.rest_10_), channel_id=1, source_target_pairs={{0,8},{8,0},{16,24},{24,16},{1,9},{9,1},{17,25},{25,17},{2,10},{10... | collective-permute-start | bytes 1867784 | tf_op jit(solution)/shard_map/ppermute | solution.py:657
  (39 other events, 355.5 us)
